TPU v7x, 32 devices: a whole 2x2x4 slice. The times are simulated.
32 devices in a mesh: expert: 4 (over x, core), fsdp: 8 (over z, y).
Axes of the slice: x: 2, y: 2, z: 4, core: 2. Of those that a mesh axis runs over, the one named last changes fastest.
Arguments:
- momentum: float32 [4, 7168, 1024], P(None, ('fsdp', 'expert')), may hold values from -6 to 6
- spectral_sq: float32 [4], P('expert'), may hold values from 10752 to 35840
Outputs:
- update: bfloat16 [4, 7168, 1024], P(None, ('fsdp', 'expert'))
All inputs are finite; a program needn't handle non-finite values.
Results may differ from a plain program's by a relative error of at most 0.0064.
Values may be sent and summed in bfloat16 or wider, within the bound.
No kernel may reach another device: no remote copies, remote signals or barrier semaphores. Data moves between devices by JAX's collectives and lax.ppermute only.
A program may use at most 64 MiB of HBM per device.

v0:
```python
import jax
import jax.numpy as jnp
from jax import lax
from jax.sharding import PartitionSpec as P

C = 7168


coef_a = 3.4445
coef_b = -4.775
coef_c = 2.0315


def transpose_dot(left_side, right_side):
    return lax.dot_general(
        left_side, right_side, (((0,), (0,)), ((), ())), preferred_element_type=jnp.float32
    )


def on_device(momentum, spectral_sq):
    gathered = lax.all_to_all(momentum, "expert", split_axis=0, concat_axis=1, tiled=True)
    scaled = (gathered / jnp.sqrt(spectral_sq)[:, None, None]).astype(jnp.bfloat16)
    own_rows = scaled[0]
    matrix_order = own_rows.shape[1]
    half_order = matrix_order // 2
    partial_value = transpose_dot(own_rows, own_rows)
    row_index = lax.broadcasted_iota(jnp.int32, (half_order, half_order), 0)
    col_index = lax.broadcasted_iota(jnp.int32, (half_order, half_order), 1)
    corner_sum = partial_value[:half_order, half_order:]
    folded = jnp.where(
        col_index >= row_index,
        partial_value[:half_order, :half_order],
        partial_value[half_order:, half_order:],
    )
    diagonal = jnp.diagonal(partial_value[half_order:, half_order:])
    summed, diag_sum = (
        lax.psum_scatter(
            jnp.concatenate([corner_sum, folded], 0), "fsdp", scatter_dimension=0, tiled=True
        ),
        lax.psum_scatter(diagonal, "fsdp", scatter_dimension=0, tiled=True),
    )
    stacked, diag_all = (
        lax.all_gather(summed.astype(jnp.bfloat16), "fsdp", axis=0, tiled=True),
        lax.all_gather(diag_sum.astype(jnp.bfloat16), "fsdp", axis=0, tiled=True),
    )
    corner = stacked[:half_order]
    packed = stacked[half_order:]
    first_block = jnp.where(col_index >= row_index, packed, packed.T)
    second_block = jnp.where(
        row_index > col_index, packed, jnp.where(row_index < col_index, packed.T, diag_all[None, :])
    )
    top_rows = jnp.concatenate([first_block, corner], 1)
    bottom_rows = jnp.concatenate([corner.T, second_block], 1)
    rounded = jnp.concatenate([top_rows, bottom_rows], 0)
    product = jnp.dot(rounded, rounded, preferred_element_type=jnp.float32)
    polynomial = (coef_b * rounded.astype(jnp.float32) + coef_c * product).astype(jnp.bfloat16)
    update = coef_a * own_rows.astype(jnp.float32) + jnp.dot(
        own_rows, polynomial, preferred_element_type=jnp.float32
    )
    result = (update * jnp.sqrt(jnp.float32(C))).astype(jnp.bfloat16)[None]
    return lax.all_to_all(result, "expert", split_axis=1, concat_axis=0, tiled=True)


def solution(mesh):
    return jax.shard_map(
        on_device,
        mesh=mesh,
        in_specs=(P(None, ("fsdp", "expert"), None), P("expert")),
        out_specs=P(None, ("fsdp", "expert"), None),
        check_vma=False,
    )
```

profile of v0, /device:TPU:0, one launch (start us, length us, event | category | flops | bytes accessed | tf_op | source)
XLA Modules:
  0.0 250.9 jit_solution(802980593948061121)
XLA Ops:
  6.5 4.7 %all-to-all-start = ((f32[4,224,1024]{2,1,0:T(8,128)}), f32[4,224,1024]{2,1,0:T(8,128)}, u32[]{:S(2)}, u32[]{:S(2)}) async-start(f32[4,224,1024]{2,1,0:T(8,128)} %param.2), calls=%async_computation | async-start | bytes 7340032 | tf_op jit(solution)/shard_map/all_to_all | solution.py:21
  11.3 0.0 reduce-scatter.2.cloned.1.call-start
  12.0 0.1 iota_compare_fusion.2
  12.1 0.4 copy.17
  12.5 42.0 %all-to-all-done = f32[4,224,1024]{2,1,0:T(8,128)} async-done(((f32[4,224,1024]{2,1,0:T(8,128)}), f32[4,224,1024]{2,1,0:T(8,128)}, u32[]{:S(2)}, u32[]{:S(2)}) %all-to-all-start) | async-done | bytes 3670048 | tf_op jit(solution)/shard_map/all_to_all | solution.py:21
  54.5 2.5 %divide_convert_fusion = bf16[4,224,1024]{2,1,0:T(8,128)(2,1)S(1)} fusion(f32[4,224,1024]{2,1,0:T(8,128)} %all-to-all-done, f32[]{:T(128)} %bitcast), kind=kLoop, calls=%fused_computation.3 | loop fusion | flops 1835008 | bytes 5505028 | tf_op jit(solution)/shard_map/convert_element_type | solution.py:22
  57.1 2.4 convolution_bitcast_fusion
  59.5 0.4 fusion.16
  59.9 1.5 pad_maximum_fusion
  61.5 0.0 reduce-scatter.2.cloned.1.call-update
  61.5 0.0 all-gather.2.cloned.1.call-start
  61.5 69.8 %reduce-scatter.2.cloned.1.call-done = f32[128,512]{1,0:T(8,128)} async-done(((f32[1024,512]{1,0:T(8,128)}), f32[128,512]{1,0:T(8,128)}) %reduce-scatter.2.cloned.1.call-update) | async-done | bytes 262160 | tf_op jit(solution)/shard_map/reduce_scatter | solution.py:37
  131.3 1.6 convert_element_type.33
  133.0 0.0 all-gather.2.cloned.1.call-update
  133.0 0.7 fusion.18
  134.9 4.5 %gather_fusion = f32[512]{0:T(512)S(1)} fusion(f32[512,512]{1,0:T(8,128)S(1)} %get-tuple-element.5, s32[512]{0:T(512)S(1)} %bitcast.22), kind=kCustom, calls=%fused_computation | custom fusion | bytes 8192 | tf_op jit(solution)/shard_map/jit(diagonal)/cond/branch_0_fun/gather | solution.py:35
  139.5 19.2 %all-reduce.1 = bf16[512]{0:T(512)(128)(2,1)S(1)} all-reduce(f32[512]{0:T(512)S(1)} %gather_fusion), channel_id=3, replica_groups=mesh['expert'=4,'fsdp'=8] {'fsdp'}, use_global_device_ids=true, to_apply=%region_1.2.clone | all-reduce | flops 512 | bytes 3072
  158.7 0.1 dynamic-slice.4
  158.8 0.2 dynamic-update-slice
  159.0 17.4 %all-reduce = bf16[512]{0:T(512)(128)(2,1)S(1)} all-reduce(bf16[512]{0:T(512)(128)(2,1)S(1)} %dynamic-update-slice), channel_id=1, replica_groups=mesh['expert'=4,'fsdp'=8] {'fsdp'}, use_global_device_ids=true, to_apply=%add | all-reduce | flops 512 | bytes 2048
  176.4 1.4 fusion.17
  177.8 0.2 copy.25
  178.1 1.0 copy.20
  179.1 1.2 bitcast_select_fusion
  180.3 8.1 %fusion.7 = bf16[1,896,1024]{2,1,0:T(8,128)(2,1)S(1)} fusion(bf16[896,1024]{1,0:T(8,128)(2,1)} %bitcast.25, bf16[512,512]{0,1:T(8,128)(2,1)} %get-tuple-element.9, bf16[512,512]{0,1:T(8,128)(2,1)S(1)} %get-tuple-element.11, bf16[512,512]{0,1:T(8,128)(2,1)} %copy.20, bf16[512,512]{0,1:T(8,128)(2,1)} %get-tuple-element.8), kind=kOutput, calls=%fused_computation.13 | convolution fusion | flops 4052090880 | bytes 5767168 | tf_op jit(solution)/shard_map/dot_general | solution.py:57
  188.3 4.6 %copy.27 = bf16[1,896,1024]{2,0,1:T(2,128)(2,1)} copy(bf16[1,896,1024]{2,1,0:T(8,128)(2,1)S(1)} %fusion.7) | data formatting | bytes 3670016 | tf_op jit(solution)/shard_map/broadcast_in_dim | solution.py:60
  193.0 0.6 broadcast.32
  193.5 12.6 %reduce = bf16[896,1024]{1,0:T(8,128)(2,1)} reduce(bf16[896,1,1024]{2,1,0:T(2,128)(2,1)} %bitcast.23, bf16[]{:T(256)} %broadcast.32), dimensions={1}, to_apply=%bitcast.21.reduce_sub_computation | reduce | bytes 3670018
  206.1 3.1 %reshape.38 = bf16[4,2,114688]{2,1,0:T(2,128)(2,1)S(1)} reshape(bf16[896,1024]{1,0:T(8,128)(2,1)} %reduce) | data formatting | bytes 3670016
  209.3 26.1 %all_to_all.21 = bf16[4,2,114688]{2,1,0:T(2,128)(2,1)} all-to-all(bf16[4,2,114688]{2,1,0:T(2,128)(2,1)S(1)} %reshape.38), channel_id=1, replica_groups=mesh['expert'=4,'fsdp'=8] {'expert'}, dimensions={0} | all-to-all | bytes 3670016 | tf_op jit(solution)/shard_map/all_to_all | solution.py:61
  235.3 4.7 %reshape.39 = bf16[896,1,1024]{2,1,0:T(2,128)(2,1)} reshape(bf16[4,2,114688]{2,1,0:T(2,128)(2,1)} %all_to_all.21) | data formatting | bytes 3670016
  240.1 4.0 %copy.24 = bf16[1,896,1024]{2,1,0:T(8,128)(2,1)} copy(bf16[1,896,1024]{2,0,1:T(2,128)(2,1)} %bitcast.24) | data formatting | bytes 3670016
  (9 shorter events, 0.0 us)
Async XLA Ops:
  6.5 48.0 %all-to-all-start = ((f32[4,224,1024]{2,1,0:T(8,128)}), f32[4,224,1024]{2,1,0:T(8,128)}, u32[]{:S(2)}, u32[]{:S(2)}) async-start(f32[4,224,1024]{2,1,0:T(8,128)} %param.2), calls=%async_computation | async-start | bytes 7340032 | tf_op jit(solution)/shard_map/all_to_all | solution.py:21
  11.3 120.1 %reduce-scatter.2.cloned.1.call-start = ((), (), s32[]{:S(2)}) async-start(), calls=%async_computation.3 | async-start | bytes 2359296 | tf_op jit(solution)/shard_map/reduce_scatter | solution.py:37
  57.1 2.4 copy-start.1
  59.9 73.1 %copy-start.2 = (u32[32]{0:T(128)S(1)}, u32[32]{0:T(128)}, u32[]{:S(2)}) copy-start(u32[32]{0:T(128)} %constant.29) | copy-start | bytes 388
  61.5 114.9 %all-gather.2.cloned.1.call-start = ((), (), s32[]{:S(2)}) async-start(), calls=%async_computation.4 | async-start | bytes 1179648 | tf_op jit(solution)/shard_map/all_gather | solution.py:43
  176.4 2.7 %copy-start = (bf16[1024,512]{1,0:T(8,128)(2,1)S(1)}, bf16[1024,512]{1,0:T(8,128)(2,1)}, u32[]{:S(2)}) copy-start(bf16[1024,512]{1,0:T(8,128)(2,1)} %all-gather.2.cloned.1.call-done) | copy-start | bytes 3145732
Sparse Core Ops, SparseCore 0:
  61.6 69.7 reduce-scatter.1
  133.5 39.3 all-gather.1
where the time goes:
time: 251 us
  waiting for transfers between devices  112 us (45%)
  blocking collectives  62.7 us (25%)
  local copies, waits for them, and re-layouts  25.5 us (10%)
  other arithmetic  19.9 us (8%)
  between operations  15.5 us (6%)
  matrix products  10.5 us (4%)
  starting transfers between devices  4.83 us (2%)
    reduce_scatter x1, waiting for transfers between devices, on_device(): lax.psum_scatter(jnp.concatenate([corner_sum, folded], 0), 'fsdp', scatte...  69.8 us
    all_to_all x1, waiting for transfers between devices, on_device(): lax.all_to_all(momentum, 'expert', split_axis=0, concat_axis=1, tiled=True)  42 us
    unnamed x2, blocking collectives  36.7 us
    all_to_all x1, blocking collectives, on_device(): lax.all_to_all(result, 'expert', split_axis=1, concat_axis=0, tiled=True)  26.1 us
    unnamed x15, local copies, waits for them, and re-layouts  13.5 us
    unnamed x1, other arithmetic  12.6 us
    dot_general x1, matrix products, on_device(): jnp.dot(own_rows, polynomial, preferred_element_type=jnp.float32)  8.07 us
  transfers between devices with their start and end apart: 3, of which 2 were waited for; matrix products, arithmetic and copies ran while one was open for 2% of the time, Pallas kernels for 0%

commit v1 on v0

v1 whole, which is shorter than its diff:
```python
import functools

import jax
import jax.numpy as jnp
from jax import lax
from jax.experimental import pallas as pl
from jax.experimental.pallas import tpu as pltpu
from jax.sharding import PartitionSpec as P

coef_a = 3.4445
coef_b = -4.775
coef_c = 2.0315

TILE = 128
PAD = 16
VMEM = pl.BlockSpec(memory_space=pltpu.VMEM)
SMEM = pl.BlockSpec(memory_space=pltpu.SMEM)


def block_table(tiles):
    table = [(i, j) for i in range(tiles) for j in range(i + 1, tiles)]
    return table + [(i, i) for i in range(0, tiles, 2)]


def contract_rows(left, right):
    return lax.dot_general(
        left, right, (((0,), (0,)), ((), ())), preferred_element_type=jnp.float32
    )


def tile_iota():
    rows = lax.broadcasted_iota(jnp.int32, (TILE, TILE), 0)
    cols = lax.broadcasted_iota(jnp.int32, (TILE, TILE), 1)
    return rows, cols


def gram_kernel(core_ref, inverse_ref, *refs):
    *row_refs, keep_ref, send_ref, packed = refs
    order = row_refs[0].shape[1]
    tiles = order // TILE
    table = block_table(tiles)
    place = {pair: index for index, pair in enumerate(table)}
    half_rows = packed.shape[1] - PAD
    per_half = half_rows // TILE
    inverse = inverse_ref[0]
    rows, cols = tile_iota()

    def put(index, value):
        half, slot = divmod(index, per_half)
        packed[half, pl.ds(slot * TILE, TILE), :] = value

    diagonals = []
    for panel in range(tiles // 2):
        start = 2 * panel * TILE
        total = None
        for ref in row_refs:
            part = contract_rows(ref[:, start : start + 2 * TILE], ref[:, start:])
            total = part if total is None else total + part
        total = total * inverse
        for side in range(2):
            i = 2 * panel + side
            for j in range(i + 1, tiles):
                at = j * TILE - start
                put(place[i, j], total[side * TILE : (side + 1) * TILE, at : at + TILE])
        first, second = total[:TILE, :TILE], total[TILE:, TILE : 2 * TILE]
        put(place[2 * panel, 2 * panel], jnp.where(cols >= rows, first, second))
        diagonals.append(jnp.sum(jnp.where(rows == cols, second, 0.0), axis=0, keepdims=True))
    tail = jnp.concatenate(
        diagonals + [jnp.zeros((PAD - len(diagonals), TILE), jnp.float32)], axis=0
    )
    for half in range(2):
        packed[half, pl.ds(half_rows, PAD), :] = tail
    core = core_ref[0]
    keep_ref[...] = packed[core]
    send_ref[...] = packed[1 - core].astype(jnp.bfloat16)


def split_kernel(place_ref, keep_ref, recv_ref, own_ref, *send_refs):
    parts = len(send_refs) + 1
    size = own_ref.shape[0] - PAD
    place = place_ref[0]
    tail = keep_ref[pl.ds(parts * size, PAD), :] + recv_ref[pl.ds(parts * size, PAD), :].astype(
        jnp.float32
    )
    for mask in range(parts):
        at = pl.ds(pl.multiple_of((place ^ mask) * size, size), size)
        total = keep_ref[at, :] + recv_ref[at, :].astype(jnp.float32)
        out = own_ref if mask == 0 else send_refs[mask - 1]
        out[pl.ds(0, size), :] = total.astype(out.dtype)
        out[pl.ds(size, PAD), :] = tail.astype(out.dtype)


def polynomial_kernel(place_ref, *refs):
    *shard_refs, out_ref, packed, gram = refs
    parts = len(shard_refs) // 2
    size = shard_refs[0].shape[0] - PAD
    order = out_ref.shape[0]
    table = block_table(order // TILE)
    place, core = place_ref[0], place_ref[1]
    for side in range(2):
        for mask in range(parts):
            at = ((core ^ side) * parts + (place ^ mask)) * size
            packed[pl.ds(pl.multiple_of(at, size), size), :] = shard_refs[side * parts + mask][
                pl.ds(0, size), :
            ]
    tail = shard_refs[0][pl.ds(size, PAD), :].astype(jnp.float32)
    rows, cols = tile_iota()
    for index, (i, j) in enumerate(table):
        tile = packed[pl.ds(index * TILE, TILE), :]
        if i != j:
            gram[pl.ds(i * TILE, TILE), pl.ds(j * TILE, TILE)] = tile
            gram[pl.ds(j * TILE, TILE), pl.ds(i * TILE, TILE)] = tile.T
        else:
            wide = tile.astype(jnp.float32)
            flipped = wide.T
            first = jnp.where(cols >= rows, wide, flipped)
            diagonal = jnp.broadcast_to(tail[i // 2 : i // 2 + 1, :], (TILE, TILE))
            second = jnp.where(rows > cols, wide, jnp.where(rows < cols, flipped, diagonal))
            a, b = pl.ds(i * TILE, TILE), pl.ds((i + 1) * TILE, TILE)
            gram[a, a] = first.astype(jnp.bfloat16)
            gram[b, b] = second.astype(jnp.bfloat16)
    step = 2 * TILE
    for at in range(0, order, step):
        square = jnp.dot(gram[pl.ds(at, step), :], gram[...], preferred_element_type=jnp.float32)
        out_ref[pl.ds(at, step), :] = (
            coef_b * gram[pl.ds(at, step), :].astype(jnp.float32) + coef_c * square
        ).astype(jnp.bfloat16)


def call(kernel, name, out, in_specs, scratch, flops):
    return pl.pallas_call(
        kernel,
        name=name,
        out_shape=out,
        in_specs=in_specs,
        out_specs=jax.tree.map(lambda _: VMEM, out),
        scratch_shapes=scratch,
        cost_estimate=pl.CostEstimate(flops=flops, bytes_accessed=4 << 20, transcendentals=0),
        compiler_params=pltpu.CompilerParams(vmem_limit_bytes=40 << 20),
    )


def on_device(experts, pieces, height, momentum, spectral_sq):
    axes = ("expert", "fsdp")
    e, f = lax.axis_index("expert"), lax.axis_index("fsdp")
    core, low, place = e & 1, f & 1, f >> 1
    own = (e & ~1) + low
    parts = pieces // 2
    count, order = momentum.shape[1:]

    def exchange(value, e_mask, f_mask):
        pairs = [
            (k * pieces + i, (k ^ e_mask) * pieces + (i ^ f_mask))
            for k in range(experts)
            for i in range(pieces)
        ]
        return lax.ppermute(value, axes, pairs)

    def other_core(value):
        return exchange(value, 1, 0)

    def to_expert(value, mask):
        return exchange(value, mask & ~1, mask & 1)

    def to_place(value, mask):
        return exchange(value, 0, mask << 1)

    def rows_of(mask):
        block = lax.dynamic_index_in_dim(momentum, own ^ mask, 0, keepdims=False)
        return block.astype(jnp.bfloat16)

    masks = list(range(experts - 1, 0, -1))
    received = {mask: to_expert(rows_of(mask), mask) for mask in masks}
    received[0] = rows_of(0)
    square = jnp.where(core == low, spectral_sq, other_core(spectral_sq))
    blocks = [received[mask] for mask in range(experts)]
    gram_rows = blocks if count % 16 == 0 else [jnp.concatenate(blocks, 0)]

    tiles = order // TILE
    half = len(block_table(tiles)) * TILE // 2
    f32, bf16 = jnp.float32, jnp.bfloat16
    shape = jax.ShapeDtypeStruct
    keep, send = call(
        gram_kernel,
        "gram",
        (shape((half + PAD, TILE), f32), shape((half + PAD, TILE), bf16)),
        [SMEM, SMEM] + [VMEM] * len(gram_rows),
        [pltpu.VMEM((2, half + PAD, TILE), f32)],
        experts * count * order * order,
    )(core.reshape(1), 1.0 / square, *gram_rows)
    size = half // parts
    own_part, *sends = call(
        split_kernel,
        "split",
        (shape((size + PAD, TILE), f32),) + (shape((size + PAD, TILE), bf16),) * (parts - 1),
        [SMEM, VMEM, VMEM],
        [],
        half * TILE,
    )(place.reshape(1), keep, other_core(send))
    order_of = list(range(parts - 1, 0, -1))
    arrived = {mask: to_place(sends[mask - 1], mask) for mask in order_of}
    total = own_part
    for mask in range(1, parts):
        total = total + arrived[mask].astype(f32)
    shard = total.astype(bf16)
    shards = {mask: to_place(shard, mask) for mask in order_of}
    shards[0] = shard
    here = [shards[mask] for mask in range(parts)]
    there = [other_core(value) for value in here]
    polynomial = call(
        polynomial_kernel,
        "polynomial",
        shape((order, order), bf16),
        [SMEM] + [VMEM] * (2 * parts),
        [pltpu.VMEM((2 * half, TILE), bf16), pltpu.VMEM((order, order), bf16)],
        2 * order**3,
    )(jnp.stack([place, core]), *here, *there)
    scale = (jnp.sqrt(jnp.float32(height)) * lax.rsqrt(square))[0]

    def update_of(mask):
        rows = received[mask]
        product = jnp.dot(rows, polynomial, preferred_element_type=f32)
        return ((coef_a * rows.astype(f32) + product) * scale).astype(bf16)

    back = {mask: to_expert(update_of(mask), mask) for mask in masks}
    back[0] = update_of(0)
    result = jnp.zeros((experts, count, order), bf16)
    for mask in [0] + masks[::-1]:
        result = lax.dynamic_update_index_in_dim(result, back[mask], own ^ mask, 0)
    return result


def solution(mesh):
    experts, pieces = mesh.shape["expert"], mesh.shape["fsdp"]

    def run(momentum, spectral_sq):
        body = functools.partial(on_device, experts, pieces, momentum.shape[1])
        return jax.shard_map(
            body,
            mesh=mesh,
            in_specs=(P(None, ("fsdp", "expert"), None), P("expert")),
            out_specs=P(None, ("fsdp", "expert"), None),
            check_vma=False,
        )(momentum, spectral_sq)

    return run
```

time: 251 us -> 90.7 us (0.36)
  blocking collectives: 62.7 us -> 0 us
  waiting for transfers between devices: 112 us -> 59.9 us
  local copies, waits for them, and re-layouts: 25.5 us -> 3.37 us
  other arithmetic: 19.9 us -> 0.15 us
  between operations: 15.5 us -> 1.54 us
  starting transfers between devices: 4.83 us -> 17.8 us
  matrix products: 10.5 us -> 2.76 us
  Pallas kernels: 0 us -> 5.06 us
    reduce_scatter x1 -> x0, waiting for transfers between devices: 69.8 us -> none  [on_device(): lax.psum_scatter(jnp.concatenate([corner_sum, folded], 0), 'fsdp', scatte...]
    ppermute x0 -> x18, waiting for transfers between devices: none -> 59.9 us  [exchange(): return lax.ppermute(value, axes, pairs)]
    all_to_all x1 -> x0, waiting for transfers between devices: 42 us -> none  [on_device(): lax.all_to_all(momentum, 'expert', split_axis=0, concat_axis=1, tiled=True)]
    unnamed x2 -> x0, blocking collectives: 36.7 us -> none
    all_to_all x1 -> x0, blocking collectives: 26.1 us -> none  [on_device(): lax.all_to_all(result, 'expert', split_axis=1, concat_axis=0, tiled=True)]
    ppermute x0 -> x18, starting transfers between devices: none -> 17.8 us  [exchange(): return lax.ppermute(value, axes, pairs)]
    unnamed x15 -> x6, local copies, waits for them, and re-layouts: 13.5 us -> 0.02 us
    unnamed x1 -> x0, other arithmetic: 12.6 us -> none
  transfers between devices with their start and end apart: 3 -> 18, of which waited for: 2 -> 14; matrix products, arithmetic and copies ran while one was open for 2% -> 3% of each run, Pallas kernels for 0% -> 0%
where the time goes in v1:
time: 90.7 us; the launch traced here: 90.6 us
  waiting for transfers between devices  59.9 us (66%)
  starting transfers between devices  17.8 us (20%)
  Pallas kernels  5.06 us (6%)
  local copies, waits for them, and re-layouts  3.37 us (4%)
  matrix products  2.76 us (3%)
  between operations  1.54 us (2%)
    ppermute x18, waiting for transfers between devices, exchange(): return lax.ppermute(value, axes, pairs)  59.9 us
    ppermute x18, starting transfers between devices, exchange(): return lax.ppermute(value, axes, pairs)  17.8 us
    pallas_call x1, Pallas kernels, on_device(): call(polynomial_kernel, 'polynomial', shape((order, order), bf16), [SMEM]...  3.22 us
    dot_general x4, matrix products, update_of(): product = jnp.dot(rows, polynomial, preferred_element_type=f32)  2.76 us
    convert_element_type x1, local copies, waits for them, and re-layouts, rows_of(): return block.astype(jnp.bfloat16)  2.26 us
  transfers between devices with their start and end apart: 18, of which 14 were waited for; matrix products, arithmetic and copies ran while one was open for 3% of the time, Pallas kernels for 0%

profile of v1, /device:TPU:0, one launch (start us, length us, event | category | flops | bytes accessed | tf_op | source)
XLA Modules:
  0.0 90.6 jit_solution(9431480775249492558)
XLA Ops:
  0.0 2.3 %fusion.7 = (bf16[224,1024]{1,0:T(8,128)(2,1)S(1)}, bf16[224,1024]{1,0:T(8,128)(2,1)S(1)}, bf16[224,1024]{1,0:T(8,128)(2,1)S(1)}, bf16[224,1024]{1,0:T(8,128)(2,1)S(1)}) fusion(f32[4,224,1024]{2,1,0:T(8,128)} %param.2, s32[]{:T(128)S(6)} %select_n.31, s32[]{:T(128)S(6)} %select_n.29, s32[]{:T(128)S(6)} %select_n.26, s32[]{:T(128)S(6)} %select_n.30), kind=kLoop, calls=%fused_computation.15 | loop fusion | bytes 3670032 | tf_op jit(solution)/shard_map/convert_element_type | solution.py:170
  2.3 4.0 %collective-permute-start.3 = (bf16[224,1024]{1,0:T(8,128)(2,1)S(1)}, bf16[224,1024]{1,0:T(8,128)(2,1)S(1)}, u32[]{:S(2)}, u32[]{:S(2)}) collective-permute-start(bf16[224,1024]{1,0:T(8,128)(2,1)S(1)} %get-tuple-element.17), channel_id=1, source_target_pairs={{0,17},{1,16},{2,19},{3,18},{4,21},{5,20},{6,23},{7,22},{8,25},{9,... | collective-permute-start | bytes 1376264 | tf_op jit(solution)/shard_map/ppermute | solution.py:157
  6.3 0.5 collective-permute-start.1
  7.6 0.8 collective-permute-done
  9.0 8.7 %collective-permute-done.3.refs_3_ = bf16[224,1024]{1,0:T(8,128)(2,1)S(1)} collective-permute-done((bf16[224,1024]{1,0:T(8,128)(2,1)S(1)}, bf16[224,1024]{1,0:T(8,128)(2,1)S(1)}, u32[]{:S(2)}, u32[]{:S(2)}) %collective-permute-start.3) | collective-permute-done | bytes 458784 | tf_op jit(solution)/shard_map/ppermute | solution.py:157
  17.7 8.9 %collective-permute-done.1.refs_1_ = bf16[224,1024]{1,0:T(8,128)(2,1)S(1)} collective-permute-done((bf16[224,1024]{1,0:T(8,128)(2,1)S(1)}, bf16[224,1024]{1,0:T(8,128)(2,1)S(1)}, u32[]{:S(2)}, u32[]{:S(2)}) %collective-permute-start.1) | collective-permute-done | bytes 458784 | tf_op jit(solution)/shard_map/ppermute | solution.py:157
  26.6 0.3 collective-permute-done.2.refs_2_
  26.9 1.7 %gram.1 = (f32[2064,128]{1,0:T(8,128)S(1)}, bf16[2064,128]{1,0:T(8,128)(2,1)S(1)}) custom-call(s32[1]{0:T(128)} %bitcast.2.core_ref, f32[1]{0:T(128)S(6)} %div.3.inverse_ref, bf16[224,1024]{1,0:T(8,128)(2,1)S(1)} %get-tuple-element.19.refs_0_, bf16[224,1024]{1,0:T(8,128)(2,1)S(1)} %collective-permute-done.1.refs_1_, ...), custom_call_target="tpu_custom_call" | custom-call | flops 939524096 | bytes 4194304 | tf_op jit(solution)/shard_map/gram/pallas_call | solution.py:183
  28.7 1.9 %collective-permute-done.4.recv_ref = bf16[2064,128]{1,0:T(8,128)(2,1)S(1)} collective-permute-done((bf16[2064,128]{1,0:T(8,128)(2,1)S(1)}, bf16[2064,128]{1,0:T(8,128)(2,1)S(1)}, u32[]{:S(2)}, u32[]{:S(2)}) %collective-permute-start.4) | collective-permute-done | bytes 528416 | tf_op jit(solution)/shard_map/ppermute | solution.py:157
  30.7 1.6 %collective-permute-start.5 = (bf16[528,128]{1,0:T(8,128)(2,1)S(1)}, bf16[528,128]{1,0:T(8,128)(2,1)S(1)}, u32[]{:S(2)}, u32[]{:S(2)}) collective-permute-start(bf16[528,128]{1,0:T(8,128)(2,1)S(1)} %get-tuple-element.14), channel_id=1, source_target_pairs={{0,2},{1,3},{2,0},{3,1},{4,6},{5,7},{6,4},{7,5},{8,10},{9,11},{10,... | collective-permute-start | bytes 405512 | tf_op jit(solution)/shard_map/ppermute | solution.py:157
  32.4 2.6 %collective-permute-start.6 = (bf16[528,128]{1,0:T(8,128)(2,1)S(1)}, bf16[528,128]{1,0:T(8,128)(2,1)S(1)}, u32[]{:S(2)}, u32[]{:S(2)}) collective-permute-start(bf16[528,128]{1,0:T(8,128)(2,1)S(1)} %get-tuple-element.15), channel_id=1, source_target_pairs={{0,4},{1,5},{2,6},{3,7},{4,0},{5,1},{6,2},{7,3},{8,12},{9,13},{10,... | collective-permute-start | bytes 405512 | tf_op jit(solution)/shard_map/ppermute | solution.py:157
  35.2 3.3 %collective-permute-done.5 = bf16[528,128]{1,0:T(8,128)(2,1)S(1)} collective-permute-done((bf16[528,128]{1,0:T(8,128)(2,1)S(1)}, bf16[528,128]{1,0:T(8,128)(2,1)S(1)}, u32[]{:S(2)}, u32[]{:S(2)}) %collective-permute-start.5) | collective-permute-done | bytes 135200 | tf_op jit(solution)/shard_map/ppermute | solution.py:157
  38.5 7.0 %collective-permute-done.6 = bf16[528,128]{1,0:T(8,128)(2,1)S(1)} collective-permute-done((bf16[528,128]{1,0:T(8,128)(2,1)S(1)}, bf16[528,128]{1,0:T(8,128)(2,1)S(1)}, u32[]{:S(2)}, u32[]{:S(2)}) %collective-permute-start.6) | collective-permute-done | bytes 135200 | tf_op jit(solution)/shard_map/ppermute | solution.py:157
  45.6 2.5 %collective-permute-start.10 = (bf16[528,128]{1,0:T(8,128)(2,1)S(1)}, bf16[528,128]{1,0:T(8,128)(2,1)S(1)}, u32[]{:S(2)}, u32[]{:S(2)}) collective-permute-start(bf16[528,128]{1,0:T(8,128)(2,1)S(1)} %add_convert_fusion.refs_0_), channel_id=1, source_target_pairs={{0,6},{1,7},{2,4},{3,5},{4,2},{5,3},{6,0},{7,1},{8,14},{9,15},{10,... | collective-permute-start | bytes 405512 | tf_op jit(solution)/shard_map/ppermute | solution.py:157
  48.1 1.4 %collective-permute-start.9 = (bf16[528,128]{1,0:T(8,128)(2,1)S(1)}, bf16[528,128]{1,0:T(8,128)(2,1)S(1)}, u32[]{:S(2)}, u32[]{:S(2)}) collective-permute-start(bf16[528,128]{1,0:T(8,128)(2,1)S(1)} %add_convert_fusion.refs_0_), channel_id=1, source_target_pairs={{0,4},{1,5},{2,6},{3,7},{4,0},{5,1},{6,2},{7,3},{8,12},{9,13},{10,... | collective-permute-start | bytes 405512 | tf_op jit(solution)/shard_map/ppermute | solution.py:157
  49.5 0.5 collective-permute-start.8
  50.1 3.6 %collective-permute-done.10.refs_3_ = bf16[528,128]{1,0:T(8,128)(2,1)S(1)} collective-permute-done((bf16[528,128]{1,0:T(8,128)(2,1)S(1)}, bf16[528,128]{1,0:T(8,128)(2,1)S(1)}, u32[]{:S(2)}, u32[]{:S(2)}) %collective-permute-start.10) | collective-permute-done | bytes 135200 | tf_op jit(solution)/shard_map/ppermute | solution.py:157
  53.7 6.0 %collective-permute-done.9.refs_2_ = bf16[528,128]{1,0:T(8,128)(2,1)S(1)} collective-permute-done((bf16[528,128]{1,0:T(8,128)(2,1)S(1)}, bf16[528,128]{1,0:T(8,128)(2,1)S(1)}, u32[]{:S(2)}, u32[]{:S(2)}) %collective-permute-start.9) | collective-permute-done | bytes 135200 | tf_op jit(solution)/shard_map/ppermute | solution.py:157
  59.7 0.5 collective-permute-start.12
  60.4 0.7 collective-permute-done.13.refs_6_
  61.3 3.2 %polynomial.1 = bf16[1024,1024]{1,0:T(8,128)(2,1)S(1)} custom-call(s32[2]{0:T(128)S(1)} %pad_add_fusion.place_ref, bf16[528,128]{1,0:T(8,128)(2,1)S(1)} %add_convert_fusion.refs_0_, bf16[528,128]{1,0:T(8,128)(2,1)S(1)} %collective-permute-done.8.refs_1_, bf16[528,128]{1,0:T(8,128)(2,1)S(1)} %collective-permute-done.9.refs_2_, ...), custom_call_target="tpu_custom_call" | custom-call | flops 2147483648 | bytes 4194304 | tf_op jit(solution)/shard_map/polynomial/pallas_call | solution.py:210
  64.5 0.7 multiply_convert_fusion.2
  65.2 1.5 %collective-permute-start.15 = (bf16[224,1024]{1,0:T(8,128)(2,1)S(1)}, bf16[224,1024]{1,0:T(8,128)(2,1)S(1)}, u32[]{:S(2)}, u32[]{:S(2)}) collective-permute-start(bf16[224,1024]{1,0:T(8,128)(2,1)S(1)} %multiply_convert_fusion.2), channel_id=1, source_target_pairs={{0,1},{1,0},{2,3},{3,2},{4,5},{5,4},{6,7},{7,6},{8,9},{9,8},{10,11... | collective-permute-start | bytes 1376264 | tf_op jit(solution)/shard_map/ppermute | solution.py:157
  66.7 0.7 multiply_convert_fusion.1
  67.4 0.9 collective-permute-start.16
  68.2 0.7 multiply_convert_fusion
  68.9 1.3 %collective-permute-start.17 = (bf16[224,1024]{1,0:T(8,128)(2,1)S(1)}, bf16[224,1024]{1,0:T(8,128)(2,1)S(1)}, u32[]{:S(2)}, u32[]{:S(2)}) collective-permute-start(bf16[224,1024]{1,0:T(8,128)(2,1)S(1)} %multiply_convert_fusion), channel_id=1, source_target_pairs={{0,17},{1,16},{2,19},{3,18},{4,21},{5,20},{6,23},{7,22},{8,25},{9,... | collective-permute-start | bytes 1376264 | tf_op jit(solution)/shard_map/ppermute | solution.py:157
  70.5 0.7 fusion.3
  71.2 6.8 %collective-permute-done.15 = bf16[224,1024]{1,0:T(8,128)(2,1)S(1)} collective-permute-done((bf16[224,1024]{1,0:T(8,128)(2,1)S(1)}, bf16[224,1024]{1,0:T(8,128)(2,1)S(1)}, u32[]{:S(2)}, u32[]{:S(2)}) %collective-permute-start.15) | collective-permute-done | bytes 458784 | tf_op jit(solution)/shard_map/ppermute | solution.py:157
  78.0 2.8 %collective-permute-done.16 = bf16[224,1024]{1,0:T(8,128)(2,1)S(1)} collective-permute-done((bf16[224,1024]{1,0:T(8,128)(2,1)S(1)}, bf16[224,1024]{1,0:T(8,128)(2,1)S(1)}, u32[]{:S(2)}, u32[]{:S(2)}) %collective-permute-start.16) | collective-permute-done | bytes 458784 | tf_op jit(solution)/shard_map/ppermute | solution.py:157
  80.9 8.9 %collective-permute-done.17 = bf16[224,1024]{1,0:T(8,128)(2,1)S(1)} collective-permute-done((bf16[224,1024]{1,0:T(8,128)(2,1)S(1)}, bf16[224,1024]{1,0:T(8,128)(2,1)S(1)}, u32[]{:S(2)}, u32[]{:S(2)}) %collective-permute-start.17) | collective-permute-done | bytes 458784 | tf_op jit(solution)/shard_map/ppermute | solution.py:157
  89.8 0.8 bitcast_dynamic-update-slice_fusion
  (24 shorter events, 1.2 us)
Async XLA Ops:
  2.3 15.4 %collective-permute-start.3 = (bf16[224,1024]{1,0:T(8,128)(2,1)S(1)}, bf16[224,1024]{1,0:T(8,128)(2,1)S(1)}, u32[]{:S(2)}, u32[]{:S(2)}) collective-permute-start(bf16[224,1024]{1,0:T(8,128)(2,1)S(1)} %get-tuple-element.17), channel_id=1, source_target_pairs={{0,17},{1,16},{2,19},{3,18},{4,21},{5,20},{6,23},{7,22},{8,25},{9,... | collective-permute-start | bytes 1376264 | tf_op jit(solution)/shard_map/ppermute | solution.py:157
  6.3 20.3 %collective-permute-start.1 = (bf16[224,1024]{1,0:T(8,128)(2,1)S(1)}, bf16[224,1024]{1,0:T(8,128)(2,1)S(1)}, u32[]{:S(2)}, u32[]{:S(2)}) collective-permute-start(bf16[224,1024]{1,0:T(8,128)(2,1)S(1)} %get-tuple-element.18), channel_id=1, source_target_pairs={{0,1},{1,0},{2,3},{3,2},{4,5},{5,4},{6,7},{7,6},{8,9},{9,8},{10,11... | collective-permute-start | bytes 1376264 | tf_op jit(solution)/shard_map/ppermute | solution.py:157
  6.8 20.1 %collective-permute-start.2 = (bf16[224,1024]{1,0:T(8,128)(2,1)S(1)}, bf16[224,1024]{1,0:T(8,128)(2,1)S(1)}, u32[]{:S(2)}, u32[]{:S(2)}) collective-permute-start(bf16[224,1024]{1,0:T(8,128)(2,1)S(1)} %get-tuple-element.20), channel_id=1, source_target_pairs={{0,16},{1,17},{2,18},{3,19},{4,20},{5,21},{6,22},{7,23},{8,24},{9,... | collective-permute-start | bytes 1376264 | tf_op jit(solution)/shard_map/ppermute | solution.py:157
  6.9 1.4 %collective-permute-start = (f32[1]{0:T(128)}, f32[1]{0:T(128)}, u32[]{:S(2)}, u32[]{:S(2)}) collective-permute-start(f32[1]{0:T(128)} %param.3), channel_id=1, source_target_pairs={{0,8},{1,9},{2,10},{3,11},{4,12},{5,13},{6,14},{7,15},{8,0},{9,1},... | collective-permute-start | bytes 20 | tf_op jit(solution)/shard_map/ppermute | solution.py:157
  26.6 2.0 %copy-start = (bf16[224,1024]{1,0:T(8,128)(2,1)}, bf16[224,1024]{1,0:T(8,128)(2,1)S(1)}, u32[]{:S(2)}) copy-start(bf16[224,1024]{1,0:T(8,128)(2,1)S(1)} %collective-permute-done.1.refs_1_) | copy-start | bytes 1376260
  28.6 2.0 %collective-permute-start.4 = (bf16[2064,128]{1,0:T(8,128)(2,1)S(1)}, bf16[2064,128]{1,0:T(8,128)(2,1)S(1)}, u32[]{:S(2)}, u32[]{:S(2)}) collective-permute-start(bf16[2064,128]{1,0:T(8,128)(2,1)S(1)} %get-tuple-element.12), channel_id=1, source_target_pairs={{0,8},{1,9},{2,10},{3,11},{4,12},{5,13},{6,14},{7,15},{8,0},{9,1},... | collective-permute-start | bytes 1585160 | tf_op jit(solution)/shard_map/ppermute | solution.py:157
  30.7 7.7 %collective-permute-start.5 = (bf16[528,128]{1,0:T(8,128)(2,1)S(1)}, bf16[528,128]{1,0:T(8,128)(2,1)S(1)}, u32[]{:S(2)}, u32[]{:S(2)}) collective-permute-start(bf16[528,128]{1,0:T(8,128)(2,1)S(1)} %get-tuple-element.14), channel_id=1, source_target_pairs={{0,2},{1,3},{2,0},{3,1},{4,6},{5,7},{6,4},{7,5},{8,10},{9,11},{10,... | collective-permute-start | bytes 405512 | tf_op jit(solution)/shard_map/ppermute | solution.py:157
  32.4 13.2 %collective-permute-start.6 = (bf16[528,128]{1,0:T(8,128)(2,1)S(1)}, bf16[528,128]{1,0:T(8,128)(2,1)S(1)}, u32[]{:S(2)}, u32[]{:S(2)}) collective-permute-start(bf16[528,128]{1,0:T(8,128)(2,1)S(1)} %get-tuple-element.15), channel_id=1, source_target_pairs={{0,4},{1,5},{2,6},{3,7},{4,0},{5,1},{6,2},{7,3},{8,12},{9,13},{10,... | collective-permute-start | bytes 405512 | tf_op jit(solution)/shard_map/ppermute | solution.py:157
  35.0 10.6 %collective-permute-start.7 = (bf16[528,128]{1,0:T(8,128)(2,1)S(1)}, bf16[528,128]{1,0:T(8,128)(2,1)S(1)}, u32[]{:S(2)}, u32[]{:S(2)}) collective-permute-start(bf16[528,128]{1,0:T(8,128)(2,1)S(1)} %get-tuple-element.16), channel_id=1, source_target_pairs={{0,6},{1,7},{2,4},{3,5},{4,2},{5,3},{6,0},{7,1},{8,14},{9,15},{10,... | collective-permute-start | bytes 405512 | tf_op jit(solution)/shard_map/ppermute | solution.py:157
  45.6 8.1 %collective-permute-start.10 = (bf16[528,128]{1,0:T(8,128)(2,1)S(1)}, bf16[528,128]{1,0:T(8,128)(2,1)S(1)}, u32[]{:S(2)}, u32[]{:S(2)}) collective-permute-start(bf16[528,128]{1,0:T(8,128)(2,1)S(1)} %add_convert_fusion.refs_0_), channel_id=1, source_target_pairs={{0,6},{1,7},{2,4},{3,5},{4,2},{5,3},{6,0},{7,1},{8,14},{9,15},{10,... | collective-permute-start | bytes 405512 | tf_op jit(solution)/shard_map/ppermute | solution.py:157
  48.1 11.6 %collective-permute-start.9 = (bf16[528,128]{1,0:T(8,128)(2,1)S(1)}, bf16[528,128]{1,0:T(8,128)(2,1)S(1)}, u32[]{:S(2)}, u32[]{:S(2)}) collective-permute-start(bf16[528,128]{1,0:T(8,128)(2,1)S(1)} %add_convert_fusion.refs_0_), channel_id=1, source_target_pairs={{0,4},{1,5},{2,6},{3,7},{4,0},{5,1},{6,2},{7,3},{8,12},{9,13},{10,... | collective-permute-start | bytes 405512 | tf_op jit(solution)/shard_map/ppermute | solution.py:157
  49.5 10.2 %collective-permute-start.8 = (bf16[528,128]{1,0:T(8,128)(2,1)S(1)}, bf16[528,128]{1,0:T(8,128)(2,1)S(1)}, u32[]{:S(2)}, u32[]{:S(2)}) collective-permute-start(bf16[528,128]{1,0:T(8,128)(2,1)S(1)} %add_convert_fusion.refs_0_), channel_id=1, source_target_pairs={{0,2},{1,3},{2,0},{3,1},{4,6},{5,7},{6,4},{7,5},{8,10},{9,11},{10,... | collective-permute-start | bytes 405512 | tf_op jit(solution)/shard_map/ppermute | solution.py:157
  50.1 10.3 %collective-permute-start.11 = (bf16[528,128]{1,0:T(8,128)(2,1)S(1)}, bf16[528,128]{1,0:T(8,128)(2,1)S(1)}, u32[]{:S(2)}, u32[]{:S(2)}) collective-permute-start(bf16[528,128]{1,0:T(8,128)(2,1)S(1)} %add_convert_fusion.refs_0_), channel_id=1, source_target_pairs={{0,8},{1,9},{2,10},{3,11},{4,12},{5,13},{6,14},{7,15},{8,0},{9,1},... | collective-permute-start | bytes 405512 | tf_op jit(solution)/shard_map/ppermute | solution.py:157
  53.7 6.7 %collective-permute-start.14 = (bf16[528,128]{1,0:T(8,128)(2,1)S(1)}, bf16[528,128]{1,0:T(8,128)(2,1)S(1)}, u32[]{:S(2)}, u32[]{:S(2)}) collective-permute-start(bf16[528,128]{1,0:T(8,128)(2,1)S(1)} %collective-permute-done.10.refs_3_), channel_id=1, source_target_pairs={{0,8},{1,9},{2,10},{3,11},{4,12},{5,13},{6,14},{7,15},{8,0},{9,1},... | collective-permute-start | bytes 405512 | tf_op jit(solution)/shard_map/ppermute | solution.py:157
  59.7 1.4 %collective-permute-start.13 = (bf16[528,128]{1,0:T(8,128)(2,1)S(1)}, bf16[528,128]{1,0:T(8,128)(2,1)S(1)}, u32[]{:S(2)}, u32[]{:S(2)}) collective-permute-start(bf16[528,128]{1,0:T(8,128)(2,1)S(1)} %collective-permute-done.9.refs_2_), channel_id=1, source_target_pairs={{0,8},{1,9},{2,10},{3,11},{4,12},{5,13},{6,14},{7,15},{8,0},{9,1},... | collective-permute-start | bytes 405512 | tf_op jit(solution)/shard_map/ppermute | solution.py:157
  59.7 1.5 %collective-permute-start.12 = (bf16[528,128]{1,0:T(8,128)(2,1)S(1)}, bf16[528,128]{1,0:T(8,128)(2,1)S(1)}, u32[]{:S(2)}, u32[]{:S(2)}) collective-permute-start(bf16[528,128]{1,0:T(8,128)(2,1)S(1)} %collective-permute-done.8.refs_1_), channel_id=1, source_target_pairs={{0,8},{1,9},{2,10},{3,11},{4,12},{5,13},{6,14},{7,15},{8,0},{9,1},... | collective-permute-start | bytes 405512 | tf_op jit(solution)/shard_map/ppermute | solution.py:157
  60.3 4.1 %copy-start.1 = (bf16[224,1024]{1,0:T(8,128)(2,1)S(1)}, bf16[224,1024]{1,0:T(8,128)(2,1)}, u32[]{:S(2)}) copy-start(bf16[224,1024]{1,0:T(8,128)(2,1)} %copy-done) | copy-start | bytes 1376260
  65.2 12.8 %collective-permute-start.15 = (bf16[224,1024]{1,0:T(8,128)(2,1)S(1)}, bf16[224,1024]{1,0:T(8,128)(2,1)S(1)}, u32[]{:S(2)}, u32[]{:S(2)}) collective-permute-start(bf16[224,1024]{1,0:T(8,128)(2,1)S(1)} %multiply_convert_fusion.2), channel_id=1, source_target_pairs={{0,1},{1,0},{2,3},{3,2},{4,5},{5,4},{6,7},{7,6},{8,9},{9,8},{10,11... | collective-permute-start | bytes 1376264 | tf_op jit(solution)/shard_map/ppermute | solution.py:157
  67.4 13.5 %collective-permute-start.16 = (bf16[224,1024]{1,0:T(8,128)(2,1)S(1)}, bf16[224,1024]{1,0:T(8,128)(2,1)S(1)}, u32[]{:S(2)}, u32[]{:S(2)}) collective-permute-start(bf16[224,1024]{1,0:T(8,128)(2,1)S(1)} %multiply_convert_fusion.1), channel_id=1, source_target_pairs={{0,16},{1,17},{2,18},{3,19},{4,20},{5,21},{6,22},{7,23},{8,24},{9,... | collective-permute-start | bytes 1376264 | tf_op jit(solution)/shard_map/ppermute | solution.py:157
  68.9 20.8 %collective-permute-start.17 = (bf16[224,1024]{1,0:T(8,128)(2,1)S(1)}, bf16[224,1024]{1,0:T(8,128)(2,1)S(1)}, u32[]{:S(2)}, u32[]{:S(2)}) collective-permute-start(bf16[224,1024]{1,0:T(8,128)(2,1)S(1)} %multiply_convert_fusion), channel_id=1, source_target_pairs={{0,17},{1,16},{2,19},{3,18},{4,21},{5,20},{6,23},{7,22},{8,25},{9,... | collective-permute-start | bytes 1376264 | tf_op jit(solution)/shard_map/ppermute | solution.py:157
  80.9 8.9 %copy-start.2 = (bf16[4,224,1024]{2,1,0:T(8,128)(2,1)}, bf16[4,224,1024]{2,1,0:T(8,128)(2,1)S(1)}, u32[]{:S(2)}) copy-start(bf16[4,224,1024]{2,1,0:T(8,128)(2,1)S(1)} %bitcast_dynamic-update-slice_fusion.1) | copy-start | bytes 5505028

commit v2 on v1

v2 whole, which is shorter than its diff:
```python
import jax
import jax.numpy as jnp
from jax import lax
from jax.experimental import pallas as pl
from jax.experimental.pallas import tpu as pltpu
from jax.sharding import PartitionSpec as P

coef_a = 3.4445
coef_b = -4.775
coef_c = 2.0315

LIMIT = 12 << 20
TILE = 128
PAD = 16
VMEM = pl.BlockSpec(memory_space=pltpu.VMEM)
SMEM = pl.BlockSpec(memory_space=pltpu.SMEM)


def block_table(tiles):
    table = [(i, j) for i in range(tiles) for j in range(i + 1, tiles)]
    return table + [(i, i) for i in range(0, tiles, 2)]


def contract_rows(left, right):
    return lax.dot_general(
        left, right, (((0,), (0,)), ((), ())), preferred_element_type=jnp.float32
    )


def tile_iota():
    rows = lax.broadcasted_iota(jnp.int32, (TILE, TILE), 0)
    cols = lax.broadcasted_iota(jnp.int32, (TILE, TILE), 1)
    return rows, cols


def gram_kernel(core_ref, *refs):
    *row_refs, keep_ref, send_ref, packed = refs
    order = row_refs[0].shape[1]
    tiles = order // TILE
    table = block_table(tiles)
    place = {pair: index for index, pair in enumerate(table)}
    half_rows = packed.shape[1] - PAD
    per_half = half_rows // TILE
    rows, cols = tile_iota()

    def put(index, value):
        half, slot = divmod(index, per_half)
        packed[half, pl.ds(slot * TILE, TILE), :] = value

    diagonals = []
    for panel in range(tiles // 2):
        start = 2 * panel * TILE
        total = None
        for ref in row_refs:
            part = contract_rows(ref[:, start : start + 2 * TILE], ref[:, start:])
            total = part if total is None else total + part
        for side in range(2):
            i = 2 * panel + side
            for j in range(i + 1, tiles):
                at = j * TILE - start
                put(place[i, j], total[side * TILE : (side + 1) * TILE, at : at + TILE])
        first, second = total[:TILE, :TILE], total[TILE:, TILE : 2 * TILE]
        put(place[2 * panel, 2 * panel], jnp.where(cols >= rows, first, second))
        diagonals.append(jnp.sum(jnp.where(rows == cols, second, 0.0), axis=0, keepdims=True))
    tail = jnp.concatenate(
        diagonals + [jnp.zeros((PAD - len(diagonals), TILE), jnp.float32)], axis=0
    )
    for half in range(2):
        packed[half, pl.ds(half_rows, PAD), :] = tail
    core = core_ref[0]
    keep_ref[...] = packed[core]
    send_ref[...] = packed[1 - core].astype(jnp.bfloat16)


def split_kernel(place_ref, keep_ref, recv_ref, own_ref, *send_refs):
    parts = len(send_refs) + 1
    size = own_ref.shape[0] - PAD
    place = place_ref[0]
    tail = keep_ref[pl.ds(parts * size, PAD), :] + recv_ref[pl.ds(parts * size, PAD), :].astype(
        jnp.float32
    )
    for mask in range(parts):
        at = pl.ds(pl.multiple_of((place ^ mask) * size, size), size)
        total = keep_ref[at, :] + recv_ref[at, :].astype(jnp.float32)
        out = own_ref if mask == 0 else send_refs[mask - 1]
        out[pl.ds(0, size), :] = total.astype(out.dtype)
        out[pl.ds(size, PAD), :] = tail.astype(out.dtype)


def total_kernel(*refs):
    *part_refs, out_ref = refs
    total = part_refs[0][...]
    for ref in part_refs[1:]:
        total = total + ref[...].astype(jnp.float32)
    out_ref[...] = total.astype(jnp.bfloat16)


def round_kernel(inverse_ref, *refs):
    *part_refs, out_ref, shard_ref = refs
    total = part_refs[0][...]
    for ref in part_refs[1:]:
        total = total + ref[...].astype(jnp.float32)
    rounded = (total * inverse_ref[0]).astype(jnp.bfloat16)
    out_ref[...] = rounded
    shard_ref[...] = rounded[: shard_ref.shape[0]]


def unpack(place_ref, tail_ref, shard_refs, packed, gram):
    parts = len(shard_refs) // 2
    tiles = gram.shape[0] // TILE
    table = block_table(tiles)
    size = len(table) * TILE // len(shard_refs)
    place, core = place_ref[0], place_ref[1]
    for side in range(2):
        for mask in range(parts):
            at = ((core ^ side) * parts + (place ^ mask)) * size
            packed[pl.ds(pl.multiple_of(at, size), size), :] = shard_refs[side * parts + mask][
                pl.ds(0, size), :
            ]
    tail = tail_ref[pl.ds(size, PAD), :].astype(jnp.float32)
    rows, cols = tile_iota()
    for index, (i, j) in enumerate(table):
        tile = packed[pl.ds(index * TILE, TILE), :]
        if i != j:
            gram[pl.ds(i * TILE, TILE), pl.ds(j * TILE, TILE)] = tile
            gram[pl.ds(j * TILE, TILE), pl.ds(i * TILE, TILE)] = tile.T
        else:
            wide = tile.astype(jnp.float32)
            flipped = wide.T
            first = jnp.where(cols >= rows, wide, flipped)
            diagonal = jnp.broadcast_to(tail[i // 2 : i // 2 + 1, :], (TILE, TILE))
            second = jnp.where(rows > cols, wide, jnp.where(rows < cols, flipped, diagonal))
            a, b = pl.ds(i * TILE, TILE), pl.ds((i + 1) * TILE, TILE)
            gram[a, a] = first.astype(jnp.bfloat16)
            gram[b, b] = second.astype(jnp.bfloat16)


def update_rows(scale_ref, row_ref, gram, out_ref, inner):
    product = jnp.dot(row_ref[...], gram[...], preferred_element_type=jnp.float32)
    inner[...] = (coef_b * row_ref[...].astype(jnp.float32) + coef_c * product).astype(jnp.bfloat16)
    product = jnp.dot(inner[...], gram[...], preferred_element_type=jnp.float32)
    out_ref[...] = (
        (coef_a * row_ref[...].astype(jnp.float32) + product) * scale_ref[0]
    ).astype(jnp.bfloat16)


def finish_kernel(place_ref, scale_ref, tail_ref, row_ref, *refs):
    *shard_refs, gram, out_ref, packed, inner = refs
    unpack(place_ref, tail_ref, shard_refs, packed, gram)
    update_rows(scale_ref, row_ref, gram, out_ref, inner)


def far_kernel(place_ref, scale_ref, tail_ref, row_ref, *refs):
    *shard_refs, out_ref, packed, inner, gram = refs
    unpack(place_ref, tail_ref, shard_refs, packed, gram)
    update_rows(scale_ref, row_ref, gram, out_ref, inner)


def cut_kernel(whole_ref, out_ref):
    out_ref[...] = whole_ref[pl.ds(0, out_ref.shape[0]), :]


def update_kernel(scale_ref, gram, row_ref, out_ref, inner):
    update_rows(scale_ref, row_ref, gram, out_ref, inner)


def place_kernel(place_ref, *refs):
    *block_refs, out_ref, sems = refs
    copies = [
        pltpu.make_async_copy(block, out_ref.at[place_ref[mask]], sems.at[mask])
        for mask, block in enumerate(block_refs)
    ]
    for copy in copies:
        copy.start()
    for copy in copies:
        copy.wait()


def call(kernel, out, in_specs, scratch, flops):
    return pl.pallas_call(
        kernel,
        out_shape=out,
        in_specs=in_specs,
        out_specs=jax.tree.map(lambda _: VMEM, out),
        scratch_shapes=scratch,
        cost_estimate=pl.CostEstimate(flops=int(flops), bytes_accessed=4 << 20, transcendentals=0),
        compiler_params=pltpu.CompilerParams(vmem_limit_bytes=LIMIT),
    )


def on_device(experts, pieces, height, momentum, spectral_sq):
    axes = ("expert", "fsdp")
    e, f = lax.axis_index("expert"), lax.axis_index("fsdp")
    core, low, place = e & 1, f & 1, f >> 1
    own = (e & ~1) + low
    parts = pieces // 2
    count, order = momentum.shape[1:]

    def exchange(value, e_mask, f_mask):
        pairs = [
            (k * pieces + i, (k ^ e_mask) * pieces + (i ^ f_mask))
            for k in range(experts)
            for i in range(pieces)
        ]
        return lax.ppermute(value, axes, pairs)

    def other_core(value):
        return exchange(value, 1, 0)

    def to_expert(value, mask):
        return exchange(value, mask & ~1, mask & 1)

    def to_place(value, mask):
        return exchange(value, 0, mask << 1)

    f32, bf16 = jnp.float32, jnp.bfloat16
    shape = jax.ShapeDtypeStruct
    tiles = order // TILE
    half = len(block_table(tiles)) * TILE // 2
    size = half // parts
    corner = jnp.stack([place, core])
    places = list(range(parts - 1, 0, -1))
    far = experts - 1
    near = list(range(1, far))

    def column_sum(rows):
        rows = rows if count % PAD == 0 else [jnp.concatenate(rows, 0)]
        keep, send = call(
            gram_kernel,
            (shape((half + PAD, TILE), f32), shape((half + PAD, TILE), bf16)),
            [SMEM] + [VMEM] * len(rows),
            [pltpu.VMEM((2, half + PAD, TILE), f32)],
            len(rows) * rows[0].shape[0] * order * order,
        )(core.reshape(1), *rows)
        swapped = other_core(send)
        own_part, *sends = call(
            split_kernel,
            (shape((size + PAD, TILE), f32),) + (shape((size + PAD, TILE), bf16),) * (parts - 1),
            [SMEM, VMEM, VMEM],
            [],
            half * TILE,
        )(place.reshape(1), keep, swapped)
        arrived = []
        for mask in places:
            arrived.append(to_place(sends[mask - 1], mask))
        return [own_part] + arrived

    def gather(shard):
        here = {0: shard}
        for mask in places:
            here[mask] = to_place(shard, mask)
        there = []
        for mask in range(parts):
            there.append(other_core(here[mask]))
        return [here[mask] for mask in range(parts)] + there

    def finish(name, scale, tail, rows, shards):
        gram_shape = (order, order)
        rows_shape = shape((count, order), bf16)
        keep = name == "near"
        return call(
            finish_kernel if keep else far_kernel,
            (shape(gram_shape, bf16), rows_shape) if keep else rows_shape,
            [SMEM, SMEM] + [VMEM] * (2 + len(shards)),
            [pltpu.VMEM((2 * half, TILE), bf16), pltpu.VMEM((count, order), bf16)]
            + ([] if keep else [pltpu.VMEM(gram_shape, bf16)]),
            4 * count * order * order,
        )(corner, scale, tail, rows, *shards)

    local = [
        lax.dynamic_index_in_dim(momentum, own ^ mask, 0, keepdims=False).astype(bf16)
        for mask in range(experts)
    ]
    received = {0: local[0]}
    for mask in near:
        received[mask] = to_expert(local[mask], mask)
    far_parts = column_sum([local[far]])
    square = jnp.where(core == low, spectral_sq, other_core(spectral_sq))
    far_square = to_expert(square, far)
    far_sum = call(
        total_kernel,
        shape((size + PAD, TILE), bf16),
        [VMEM] * len(far_parts),
        [],
        size * TILE * parts,
    )(*far_parts)
    far_sum = to_expert(far_sum, far)
    near_parts = column_sum([received[mask] for mask in [0] + near])
    rounded, shard = call(
        round_kernel,
        (shape((size + PAD, TILE), bf16), shape((size, TILE), bf16)),
        [SMEM] + [VMEM] * (len(near_parts) + 1),
        [],
        size * TILE * parts,
    )(1.0 / square, *near_parts, far_sum)
    shards = gather(shard)
    far_rounded = to_expert(rounded, far)
    far_shard = call(cut_kernel, shape((size, TILE), bf16), [VMEM], [], size * TILE)(far_rounded)
    far_shards = gather(far_shard)
    height_root = jnp.sqrt(jnp.float32(height))
    scale = height_root * lax.rsqrt(square)
    far_scale = height_root * lax.rsqrt(far_square)

    back = {}
    first = near[0]
    gram, back[first] = finish("near", scale, rounded, received[first], shards)
    for mask in near[1:] + [0]:
        back[mask] = call(
            update_kernel,
            shape((count, order), bf16),
            [SMEM, VMEM, VMEM],
            [pltpu.VMEM((count, order), bf16)],
            4 * count * order * order,
        )(scale, gram, received[mask])
    for mask in near:
        back[mask] = to_expert(back[mask], mask)
    back[far] = finish("far", far_scale, far_rounded, local[far], far_shards)
    if count % PAD:
        result = jnp.zeros((experts, count, order), bf16)
        for mask in range(experts):
            result = lax.dynamic_update_index_in_dim(result, back[mask], own ^ mask, 0)
        return result
    return pl.pallas_call(
        place_kernel,
        name="place",
        out_shape=shape((experts, count, order), bf16),
        in_specs=[SMEM] + [VMEM] * experts,
        out_specs=pl.BlockSpec(memory_space=pltpu.HBM),
        scratch_shapes=[pltpu.SemaphoreType.DMA((experts,))],
        compiler_params=pltpu.CompilerParams(vmem_limit_bytes=LIMIT),
    )(own ^ jnp.arange(experts, dtype=jnp.int32), *[back[mask] for mask in range(experts)])


def solution(mesh):
    experts, pieces = mesh.shape["expert"], mesh.shape["fsdp"]

    def body(momentum, spectral_sq):
        height = momentum.shape[1] * experts * pieces
        return on_device(experts, pieces, height, momentum, spectral_sq)

    return jax.shard_map(
        body,
        mesh=mesh,
        in_specs=(P(None, ("fsdp", "expert"), None), P("expert")),
        out_specs=P(None, ("fsdp", "expert"), None),
        check_vma=False,
    )
```

time: 90.7 us -> 103 us (1.14)
  starting transfers between devices: 17.8 us -> 37 us
  waiting for transfers between devices: 59.9 us -> 44.1 us
  Pallas kernels: 5.06 us -> 13.8 us
  matrix products: 2.76 us -> 0 us
  local copies, waits for them, and re-layouts: 3.37 us -> 5.04 us
    ppermute x18 -> x30, starting transfers between devices: 17.8 us -> 37 us  [exchange(): return lax.ppermute(value, axes, pairs)]
    ppermute x18 -> x30, waiting for transfers between devices: 59.9 us -> 44.1 us  [exchange(): return lax.ppermute(value, axes, pairs)]
    pallas_call x3 -> x12, Pallas kernels: 5.06 us -> 13.8 us  [the longest x2 4.64 us: column_sum(): call(gram_kernel, (shape((half + PAD, TILE), f32), shape((half + PAD, TIL...]
    dot_general x4 -> x0, matrix products: 2.76 us -> none  [update_of(): product = jnp.dot(rows, polynomial, preferred_element_type=f32)]
    unnamed x6 -> x14, local copies, waits for them, and re-layouts: 0.02 us -> 1.83 us
  transfers between devices with their start and end apart: 18 -> 30, of which waited for: 14 -> 14; matrix products, arithmetic and copies ran while one was open for 3% -> 0% of each run, Pallas kernels for 0% -> 12%
where the time goes in v2:
time: 103 us; the launch traced here: 102 us
  waiting for transfers between devices  44.1 us (43%)
  starting transfers between devices  37 us (36%)
  Pallas kernels  13.8 us (13%)
  local copies, waits for them, and re-layouts  5.04 us (5%)
  between operations  2.23 us (2%)
    ppermute x30, waiting for transfers between devices, exchange(): return lax.ppermute(value, axes, pairs)  44.1 us
    ppermute x30, starting transfers between devices, exchange(): return lax.ppermute(value, axes, pairs)  37 us
    pallas_call x2, Pallas kernels, column_sum(): call(gram_kernel, (shape((half + PAD, TILE), f32), shape((half + PAD, TIL...  4.64 us
    pallas_call x2, Pallas kernels, finish(): call(finish_kernel if keep else far_kernel, (shape(gram_shape, bf16), row...  4.59 us
    convert_element_type x1, local copies, waits for them, and re-layouts, on_device(): lax.dynamic_index_in_dim(momentum, own ^ mask, 0, keepdims=False)  3.22 us
    pallas_call x2, Pallas kernels, on_device(): call(update_kernel, shape((count, order), bf16), [SMEM, VMEM, VMEM], [plt...  2.34 us
  transfers between devices with their start and end apart: 30, of which 14 were waited for; matrix products, arithmetic and copies ran while one was open for 0% of the time, Pallas kernels for 12%

profile of v2, /device:TPU:0, one launch (start us, length us, event | category | flops | bytes accessed | tf_op | source)
XLA Modules:
  0.0 102.2 jit_solution(13713549004804260496)
XLA Ops:
  0.0 3.2 %fusion.3 = (bf16[224,1024]{1,0:T(8,128)(2,1)S(1)}, bf16[224,1024]{1,0:T(8,128)(2,1)}, bf16[224,1024]{1,0:T(8,128)(2,1)S(1)}, bf16[224,1024]{1,0:T(8,128)(2,1)}) fusion(f32[4,224,1024]{2,1,0:T(8,128)} %param.2, s32[]{:T(128)S(6)} %select_n.26, s32[]{:T(128)S(6)} %select_n.24, s32[]{:T(128)S(6)} %select_n.23, s32[]{:T(128)S(6)} %select_n.25), kind=kLoop, calls=%fused_computation.7 | loop fusion | bytes 3670032 | tf_op jit(solution)/shard_map/convert_element_type | solution.py:271
  3.2 3.0 %collective-permute-start.1 = (bf16[224,1024]{1,0:T(8,128)(2,1)}, bf16[224,1024]{1,0:T(8,128)(2,1)}, u32[]{:S(2)}, u32[]{:S(2)}) collective-permute-start(bf16[224,1024]{1,0:T(8,128)(2,1)} %get-tuple-element.38), channel_id=1, source_target_pairs={{0,1},{1,0},{2,3},{3,2},{4,5},{5,4},{6,7},{7,6},{8,9},{9,8},{10,11... | collective-permute-start | bytes 1376264 | tf_op jit(solution)/shard_map/ppermute | solution.py:205
  6.2 1.5 %collective-permute-start.2 = (bf16[224,1024]{1,0:T(8,128)(2,1)}, bf16[224,1024]{1,0:T(8,128)(2,1)S(1)}, u32[]{:S(2)}, u32[]{:S(2)}) collective-permute-start(bf16[224,1024]{1,0:T(8,128)(2,1)} %get-tuple-element.40), channel_id=1, source_target_pairs={{0,16},{1,17},{2,18},{3,19},{4,20},{5,21},{6,22},{7,23},{8,24},{9,... | collective-permute-start | bytes 1376264 | tf_op jit(solution)/shard_map/ppermute | solution.py:205
  7.7 1.5 %shard_map.30 = (f32[2064,128]{1,0:T(8,128)S(1)}, bf16[2064,128]{1,0:T(8,128)(2,1)}) custom-call(s32[1]{0:T(128)} %bitcast.2.core_ref, bf16[224,1024]{1,0:T(8,128)(2,1)S(1)} %get-tuple-element.37.refs_0_.row_ref), custom_call_target="tpu_custom_call" | custom-call | flops 234881024 | bytes 4194304 | tf_op jit(solution)/shard_map/pallas_call | solution.py:228
  9.2 7.9 %collective-permute-done.1.refs_1_.row_ref = bf16[224,1024]{1,0:T(8,128)(2,1)} collective-permute-done((bf16[224,1024]{1,0:T(8,128)(2,1)}, bf16[224,1024]{1,0:T(8,128)(2,1)}, u32[]{:S(2)}, u32[]{:S(2)}) %collective-permute-start.1) | collective-permute-done | bytes 458784 | tf_op jit(solution)/shard_map/ppermute | solution.py:205
  17.1 1.4 %collective-permute-done.2.refs_2_.row_ref = bf16[224,1024]{1,0:T(8,128)(2,1)S(1)} collective-permute-done((bf16[224,1024]{1,0:T(8,128)(2,1)}, bf16[224,1024]{1,0:T(8,128)(2,1)S(1)}, u32[]{:S(2)}, u32[]{:S(2)}) %collective-permute-start.2) | collective-permute-done | bytes 458784 | tf_op jit(solution)/shard_map/ppermute | solution.py:205
  20.2 3.2 %shard_map.28 = (f32[2064,128]{1,0:T(8,128)S(1)}, bf16[2064,128]{1,0:T(8,128)(2,1)}) custom-call(s32[1]{0:T(128)} %bitcast.2.core_ref, bf16[224,1024]{1,0:T(8,128)(2,1)S(1)} %get-tuple-element.39.refs_0_.row_ref, bf16[224,1024]{1,0:T(8,128)(2,1)} %collective-permute-done.1.refs_1_.row_ref, bf16[224,1024]{1,0:T(8,128)(2,1)S(1)} %copy-done.5), custom_call_target="tpu_custom_call" | custom-call | flops 704643072 | bytes 4194304 | tf_op jit(solution)/shard_map/pallas_call | solution.py:228
  23.6 3.7 %collective-permute-start.8 = (bf16[528,128]{1,0:T(8,128)(2,1)S(1)}, bf16[528,128]{1,0:T(8,128)(2,1)S(1)}, u32[]{:S(2)}, u32[]{:S(2)}) collective-permute-start(bf16[528,128]{1,0:T(8,128)(2,1)S(1)} %get-tuple-element.30), channel_id=1, source_target_pairs={{0,6},{1,7},{2,4},{3,5},{4,2},{5,3},{6,0},{7,1},{8,14},{9,15},{10,... | collective-permute-start | bytes 405512 | tf_op jit(solution)/shard_map/ppermute | solution.py:205
  28.0 4.0 %collective-permute-done.8.refs_1_ = bf16[528,128]{1,0:T(8,128)(2,1)S(1)} collective-permute-done((bf16[528,128]{1,0:T(8,128)(2,1)S(1)}, bf16[528,128]{1,0:T(8,128)(2,1)S(1)}, u32[]{:S(2)}, u32[]{:S(2)}) %collective-permute-start.8) | collective-permute-done | bytes 135200 | tf_op jit(solution)/shard_map/ppermute | solution.py:205
  32.0 7.3 %collective-permute-done.9.refs_2_ = bf16[528,128]{1,0:T(8,128)(2,1)S(1)} collective-permute-done((bf16[528,128]{1,0:T(8,128)(2,1)S(1)}, bf16[528,128]{1,0:T(8,128)(2,1)S(1)}, u32[]{:S(2)}, u32[]{:S(2)}) %collective-permute-start.9) | collective-permute-done | bytes 135200 | tf_op jit(solution)/shard_map/ppermute | solution.py:205
  39.4 1.5 %collective-permute-start.11 = (bf16[528,128]{1,0:T(8,128)(2,1)S(1)}, bf16[528,128]{1,0:T(8,128)(2,1)S(1)}, u32[]{:S(2)}, u32[]{:S(2)}) collective-permute-start(bf16[528,128]{1,0:T(8,128)(2,1)S(1)} %shard_map.32), channel_id=1, source_target_pairs={{0,17},{1,16},{2,19},{3,18},{4,21},{5,20},{6,23},{7,22},{8,25},{9,... | collective-permute-start | bytes 405512 | tf_op jit(solution)/shard_map/ppermute | solution.py:205
  41.0 2.5 %collective-permute-start.4 = (bf16[528,128]{1,0:T(8,128)(2,1)S(1)}, bf16[528,128]{1,0:T(8,128)(2,1)S(1)}, u32[]{:S(2)}, u32[]{:S(2)}) collective-permute-start(bf16[528,128]{1,0:T(8,128)(2,1)S(1)} %get-tuple-element.24), channel_id=1, source_target_pairs={{0,6},{1,7},{2,4},{3,5},{4,2},{5,3},{6,0},{7,1},{8,14},{9,15},{10,... | collective-permute-start | bytes 405512 | tf_op jit(solution)/shard_map/ppermute | solution.py:205
  43.6 1.9 %collective-permute-start.6 = (bf16[528,128]{1,0:T(8,128)(2,1)S(1)}, bf16[528,128]{1,0:T(8,128)(2,1)S(1)}, u32[]{:S(2)}, u32[]{:S(2)}) collective-permute-start(bf16[528,128]{1,0:T(8,128)(2,1)S(1)} %get-tuple-element.26), channel_id=1, source_target_pairs={{0,2},{1,3},{2,0},{3,1},{4,6},{5,7},{6,4},{7,5},{8,10},{9,11},{10,... | collective-permute-start | bytes 405512 | tf_op jit(solution)/shard_map/ppermute | solution.py:205
  47.6 1.8 %collective-permute-done.4.refs_1_ = bf16[528,128]{1,0:T(8,128)(2,1)S(1)} collective-permute-done((bf16[528,128]{1,0:T(8,128)(2,1)S(1)}, bf16[528,128]{1,0:T(8,128)(2,1)S(1)}, u32[]{:S(2)}, u32[]{:S(2)}) %collective-permute-start.4) | collective-permute-done | bytes 135200 | tf_op jit(solution)/shard_map/ppermute | solution.py:205
  49.4 4.7 %collective-permute-done.5.refs_2_ = bf16[528,128]{1,0:T(8,128)(2,1)S(1)} collective-permute-done((bf16[528,128]{1,0:T(8,128)(2,1)S(1)}, bf16[528,128]{1,0:T(8,128)(2,1)S(1)}, u32[]{:S(2)}, u32[]{:S(2)}) %collective-permute-start.5) | collective-permute-done | bytes 135200 | tf_op jit(solution)/shard_map/ppermute | solution.py:205
  54.1 2.1 %collective-permute-start.14 = (bf16[512,128]{1,0:T(8,128)(2,1)S(1)}, bf16[512,128]{1,0:T(8,128)(2,1)S(1)}, u32[]{:S(2)}, u32[]{:S(2)}) collective-permute-start(bf16[512,128]{1,0:T(8,128)(2,1)S(1)} %get-tuple-element.34.refs_0_), channel_id=1, source_target_pairs={{0,6},{1,7},{2,4},{3,5},{4,2},{5,3},{6,0},{7,1},{8,14},{9,15},{10,... | collective-permute-start | bytes 393224 | tf_op jit(solution)/shard_map/ppermute | solution.py:205
  56.2 2.4 %collective-permute-start.12 = (bf16[512,128]{1,0:T(8,128)(2,1)S(1)}, bf16[512,128]{1,0:T(8,128)(2,1)S(1)}, u32[]{:S(2)}, u32[]{:S(2)}) collective-permute-start(bf16[512,128]{1,0:T(8,128)(2,1)S(1)} %get-tuple-element.34.refs_0_), channel_id=1, source_target_pairs={{0,2},{1,3},{2,0},{3,1},{4,6},{5,7},{6,4},{7,5},{8,10},{9,11},{10,... | collective-permute-start | bytes 393224 | tf_op jit(solution)/shard_map/ppermute | solution.py:205
  58.6 1.5 %collective-permute-start.22 = (bf16[528,128]{1,0:T(8,128)(2,1)S(1)}, bf16[528,128]{1,0:T(8,128)(2,1)S(1)}, u32[]{:S(2)}, u32[]{:S(2)}) collective-permute-start(bf16[528,128]{1,0:T(8,128)(2,1)S(1)} %get-tuple-element.33.tail_ref), channel_id=1, source_target_pairs={{0,17},{1,16},{2,19},{3,18},{4,21},{5,20},{6,23},{7,22},{8,25},{9,... | collective-permute-start | bytes 405512 | tf_op jit(solution)/shard_map/ppermute | solution.py:205
  60.1 2.3 %collective-permute-done.14.refs_3_ = bf16[512,128]{1,0:T(8,128)(2,1)S(1)} collective-permute-done((bf16[512,128]{1,0:T(8,128)(2,1)S(1)}, bf16[512,128]{1,0:T(8,128)(2,1)S(1)}, u32[]{:S(2)}, u32[]{:S(2)}) %collective-permute-start.14) | collective-permute-done | bytes 131104 | tf_op jit(solution)/shard_map/ppermute | solution.py:205
  62.4 4.9 %collective-permute-done.13.refs_2_ = bf16[512,128]{1,0:T(8,128)(2,1)S(1)} collective-permute-done((bf16[512,128]{1,0:T(8,128)(2,1)S(1)}, bf16[512,128]{1,0:T(8,128)(2,1)S(1)}, u32[]{:S(2)}, u32[]{:S(2)}) %collective-permute-start.13) | collective-permute-done | bytes 131104 | tf_op jit(solution)/shard_map/ppermute | solution.py:205
  68.8 2.6 %shard_map.34 = (bf16[1024,1024]{1,0:T(8,128)(2,1)S(1)}, bf16[224,1024]{1,0:T(8,128)(2,1)S(1)}) custom-call(s32[2]{0:T(128)S(1)} %pad_add_fusion.place_ref, f32[1]{0:T(128)S(6)} %mul.6.scale_ref, bf16[528,128]{1,0:T(8,128)(2,1)S(1)} %get-tuple-element.33.tail_ref, bf16[224,1024]{1,0:T(8,128)(2,1)} %collective-permute-done.1.refs_1_.row_ref, ...), custom_call_target="tpu_custom_call" | custom-call | flops 939524096 | bytes 4194304 | tf_op jit(solution)/shard_map/pallas_call | solution.py:261
  71.4 1.2 %shard_map.36 = bf16[224,1024]{1,0:T(8,128)(2,1)S(1)} custom-call(f32[1]{0:T(128)S(6)} %mul.6.scale_ref, bf16[1024,1024]{1,0:T(8,128)(2,1)S(1)} %get-tuple-element.35.gram, bf16[224,1024]{1,0:T(8,128)(2,1)S(1)} %copy-done.6), custom_call_target="tpu_custom_call" | custom-call | flops 939524096 | bytes 4194304 | tf_op jit(solution)/shard_map/pallas_call | solution.py:308
  73.2 1.5 %collective-permute-start.19 = (bf16[224,1024]{1,0:T(8,128)(2,1)S(1)}, bf16[224,1024]{1,0:T(8,128)(2,1)S(1)}, u32[]{:S(2)}, u32[]{:S(2)}) collective-permute-start(bf16[224,1024]{1,0:T(8,128)(2,1)S(1)} %get-tuple-element.36), channel_id=1, source_target_pairs={{0,1},{1,0},{2,3},{3,2},{4,5},{5,4},{6,7},{7,6},{8,9},{9,8},{10,11... | collective-permute-start | bytes 1376264 | tf_op jit(solution)/shard_map/ppermute | solution.py:205
  74.7 8.8 %collective-permute-start.21 = (f32[1]{0:T(128)}, f32[1]{0:T(128)}, u32[]{:S(2)}, u32[]{:S(2)}) collective-permute-start(f32[1]{0:T(128)} %select_n.22), channel_id=1, source_target_pairs={{0,17},{1,16},{2,19},{3,18},{4,21},{5,20},{6,23},{7,22},{8,25},{9,... | collective-permute-start | bytes 20 | tf_op jit(solution)/shard_map/ppermute | solution.py:205
  83.5 1.8 %collective-permute-start.25 = (bf16[512,128]{1,0:T(8,128)(2,1)S(1)}, bf16[512,128]{1,0:T(8,128)(2,1)S(1)}, u32[]{:S(2)}, u32[]{:S(2)}) collective-permute-start(bf16[512,128]{1,0:T(8,128)(2,1)S(1)} %shard_map.37.refs_0_), channel_id=1, source_target_pairs={{0,6},{1,7},{2,4},{3,5},{4,2},{5,3},{6,0},{7,1},{8,14},{9,15},{10,... | collective-permute-start | bytes 393224 | tf_op jit(solution)/shard_map/ppermute | solution.py:205
  85.3 1.2 %collective-permute-done.21 = f32[1]{0:T(128)} collective-permute-done((f32[1]{0:T(128)}, f32[1]{0:T(128)}, u32[]{:S(2)}, u32[]{:S(2)}) %collective-permute-start.21) | collective-permute-done | bytes 36 | tf_op jit(solution)/shard_map/ppermute | solution.py:205
  86.5 2.3 %collective-permute-start.23 = (bf16[512,128]{1,0:T(8,128)(2,1)S(1)}, bf16[512,128]{1,0:T(8,128)(2,1)S(1)}, u32[]{:S(2)}, u32[]{:S(2)}) collective-permute-start(bf16[512,128]{1,0:T(8,128)(2,1)S(1)} %shard_map.37.refs_0_), channel_id=1, source_target_pairs={{0,2},{1,3},{2,0},{3,1},{4,6},{5,7},{6,4},{7,5},{8,10},{9,11},{10,... | collective-permute-start | bytes 393224 | tf_op jit(solution)/shard_map/ppermute | solution.py:205
  88.8 2.9 %collective-permute-done.25.refs_3_ = bf16[512,128]{1,0:T(8,128)(2,1)S(1)} collective-permute-done((bf16[512,128]{1,0:T(8,128)(2,1)S(1)}, bf16[512,128]{1,0:T(8,128)(2,1)S(1)}, u32[]{:S(2)}, u32[]{:S(2)}) %collective-permute-start.25) | collective-permute-done | bytes 131104 | tf_op jit(solution)/shard_map/ppermute | solution.py:205
  91.7 4.3 %collective-permute-done.24.refs_2_ = bf16[512,128]{1,0:T(8,128)(2,1)S(1)} collective-permute-done((bf16[512,128]{1,0:T(8,128)(2,1)S(1)}, bf16[512,128]{1,0:T(8,128)(2,1)S(1)}, u32[]{:S(2)}, u32[]{:S(2)}) %collective-permute-start.24) | collective-permute-done | bytes 131104 | tf_op jit(solution)/shard_map/ppermute | solution.py:205
  97.2 1.2 %shard_map.35.refs_0_ = bf16[224,1024]{1,0:T(8,128)(2,1)S(1)} custom-call(f32[1]{0:T(128)S(6)} %mul.6.scale_ref, bf16[1024,1024]{1,0:T(8,128)(2,1)S(1)} %get-tuple-element.35.gram, bf16[224,1024]{1,0:T(8,128)(2,1)S(1)} %copy-done.3), custom_call_target="tpu_custom_call" | custom-call | flops 939524096 | bytes 4194304 | tf_op jit(solution)/shard_map/pallas_call | solution.py:308
  98.4 2.0 %shard_map.38.refs_3_ = bf16[224,1024]{1,0:T(8,128)(2,1)S(1)} custom-call(s32[2]{0:T(128)S(1)} %pad_add_fusion.place_ref, f32[1]{0:T(128)S(6)} %mul.7.scale_ref, bf16[528,128]{1,0:T(8,128)(2,1)S(1)} %collective-permute-done.22.whole_ref.tail_ref, bf16[224,1024]{1,0:T(8,128)(2,1)S(1)} %copy-done.1, bf16[512,128]{1,0:T(8,128)(2,1)S(1)} %shard_map.37.refs_0_, ...), custom_call_target="tpu_custom_call" | custom-call | flops 939524096 | bytes 4194304 | tf_op jit(solution)/shard_map/pallas_call | solution.py:261
  100.4 1.8 %place.1 = bf16[4,224,1024]{2,1,0:T(8,128)(2,1)} custom-call(s32[4]{0:T(128)S(1)} %iota_xor_fusion.place_ref, bf16[224,1024]{1,0:T(8,128)(2,1)S(1)} %shard_map.35.refs_0_, bf16[224,1024]{1,0:T(8,128)(2,1)S(1)} %collective-permute-done.19.refs_1_, bf16[224,1024]{1,0:T(8,128)(2,1)S(1)} %collective-permute-done.20.refs_2_, bf16[224,1024]{1,0:T(8,128)(2,1)S(1)} %shard_map.38.refs_3_), custom_call_target="tpu_custom_call" | custom-call | tf_op jit(solution)/shard_map/place/pallas_call | solution.py:323
  (57 shorter events, 6.4 us)
Async XLA Ops:
  3.2 13.8 %collective-permute-start.1 = (bf16[224,1024]{1,0:T(8,128)(2,1)}, bf16[224,1024]{1,0:T(8,128)(2,1)}, u32[]{:S(2)}, u32[]{:S(2)}) collective-permute-start(bf16[224,1024]{1,0:T(8,128)(2,1)} %get-tuple-element.38), channel_id=1, source_target_pairs={{0,1},{1,0},{2,3},{3,2},{4,5},{5,4},{6,7},{7,6},{8,9},{9,8},{10,11... | collective-permute-start | bytes 1376264 | tf_op jit(solution)/shard_map/ppermute | solution.py:205
  6.2 12.2 %collective-permute-start.2 = (bf16[224,1024]{1,0:T(8,128)(2,1)}, bf16[224,1024]{1,0:T(8,128)(2,1)S(1)}, u32[]{:S(2)}, u32[]{:S(2)}) collective-permute-start(bf16[224,1024]{1,0:T(8,128)(2,1)} %get-tuple-element.40), channel_id=1, source_target_pairs={{0,16},{1,17},{2,18},{3,19},{4,20},{5,21},{6,22},{7,23},{8,24},{9,... | collective-permute-start | bytes 1376264 | tf_op jit(solution)/shard_map/ppermute | solution.py:205
  9.2 14.2 %collective-permute-start.7 = (bf16[2064,128]{1,0:T(8,128)(2,1)}, bf16[2064,128]{1,0:T(8,128)(2,1)S(1)}, u32[]{:S(2)}, u32[]{:S(2)}) collective-permute-start(bf16[2064,128]{1,0:T(8,128)(2,1)} %get-tuple-element.28), channel_id=1, source_target_pairs={{0,8},{1,9},{2,10},{3,11},{4,12},{5,13},{6,14},{7,15},{8,0},{9,1},... | collective-permute-start | bytes 1585160 | tf_op jit(solution)/shard_map/ppermute | solution.py:205
  23.4 17.5 %collective-permute-start.3 = (bf16[2064,128]{1,0:T(8,128)(2,1)}, bf16[2064,128]{1,0:T(8,128)(2,1)S(1)}, u32[]{:S(2)}, u32[]{:S(2)}) collective-permute-start(bf16[2064,128]{1,0:T(8,128)(2,1)} %get-tuple-element.22), channel_id=1, source_target_pairs={{0,8},{1,9},{2,10},{3,11},{4,12},{5,13},{6,14},{7,15},{8,0},{9,1},... | collective-permute-start | bytes 1585160 | tf_op jit(solution)/shard_map/ppermute | solution.py:205
  23.6 8.4 %collective-permute-start.8 = (bf16[528,128]{1,0:T(8,128)(2,1)S(1)}, bf16[528,128]{1,0:T(8,128)(2,1)S(1)}, u32[]{:S(2)}, u32[]{:S(2)}) collective-permute-start(bf16[528,128]{1,0:T(8,128)(2,1)S(1)} %get-tuple-element.30), channel_id=1, source_target_pairs={{0,6},{1,7},{2,4},{3,5},{4,2},{5,3},{6,0},{7,1},{8,14},{9,15},{10,... | collective-permute-start | bytes 405512 | tf_op jit(solution)/shard_map/ppermute | solution.py:205
  27.2 12.1 %collective-permute-start.9 = (bf16[528,128]{1,0:T(8,128)(2,1)S(1)}, bf16[528,128]{1,0:T(8,128)(2,1)S(1)}, u32[]{:S(2)}, u32[]{:S(2)}) collective-permute-start(bf16[528,128]{1,0:T(8,128)(2,1)S(1)} %get-tuple-element.31), channel_id=1, source_target_pairs={{0,4},{1,5},{2,6},{3,7},{4,0},{5,1},{6,2},{7,3},{8,12},{9,13},{10,... | collective-permute-start | bytes 405512 | tf_op jit(solution)/shard_map/ppermute | solution.py:205
  27.2 12.1 %collective-permute-start.10 = (bf16[528,128]{1,0:T(8,128)(2,1)S(1)}, bf16[528,128]{1,0:T(8,128)(2,1)S(1)}, u32[]{:S(2)}, u32[]{:S(2)}) collective-permute-start(bf16[528,128]{1,0:T(8,128)(2,1)S(1)} %get-tuple-element.32), channel_id=1, source_target_pairs={{0,2},{1,3},{2,0},{3,1},{4,6},{5,7},{6,4},{7,5},{8,10},{9,11},{10,... | collective-permute-start | bytes 405512 | tf_op jit(solution)/shard_map/ppermute | solution.py:205
  39.4 8.2 %collective-permute-start.11 = (bf16[528,128]{1,0:T(8,128)(2,1)S(1)}, bf16[528,128]{1,0:T(8,128)(2,1)S(1)}, u32[]{:S(2)}, u32[]{:S(2)}) collective-permute-start(bf16[528,128]{1,0:T(8,128)(2,1)S(1)} %shard_map.32), channel_id=1, source_target_pairs={{0,17},{1,16},{2,19},{3,18},{4,21},{5,20},{6,23},{7,22},{8,25},{9,... | collective-permute-start | bytes 405512 | tf_op jit(solution)/shard_map/ppermute | solution.py:205
  41.0 8.3 %collective-permute-start.4 = (bf16[528,128]{1,0:T(8,128)(2,1)S(1)}, bf16[528,128]{1,0:T(8,128)(2,1)S(1)}, u32[]{:S(2)}, u32[]{:S(2)}) collective-permute-start(bf16[528,128]{1,0:T(8,128)(2,1)S(1)} %get-tuple-element.24), channel_id=1, source_target_pairs={{0,6},{1,7},{2,4},{3,5},{4,2},{5,3},{6,0},{7,1},{8,14},{9,15},{10,... | collective-permute-start | bytes 405512 | tf_op jit(solution)/shard_map/ppermute | solution.py:205
  43.6 10.4 %collective-permute-start.5 = (bf16[528,128]{1,0:T(8,128)(2,1)S(1)}, bf16[528,128]{1,0:T(8,128)(2,1)S(1)}, u32[]{:S(2)}, u32[]{:S(2)}) collective-permute-start(bf16[528,128]{1,0:T(8,128)(2,1)S(1)} %get-tuple-element.25), channel_id=1, source_target_pairs={{0,4},{1,5},{2,6},{3,7},{4,0},{5,1},{6,2},{7,3},{8,12},{9,13},{10,... | collective-permute-start | bytes 405512 | tf_op jit(solution)/shard_map/ppermute | solution.py:205
  43.6 10.4 %collective-permute-start.6 = (bf16[528,128]{1,0:T(8,128)(2,1)S(1)}, bf16[528,128]{1,0:T(8,128)(2,1)S(1)}, u32[]{:S(2)}, u32[]{:S(2)}) collective-permute-start(bf16[528,128]{1,0:T(8,128)(2,1)S(1)} %get-tuple-element.26), channel_id=1, source_target_pairs={{0,2},{1,3},{2,0},{3,1},{4,6},{5,7},{6,4},{7,5},{8,10},{9,11},{10,... | collective-permute-start | bytes 405512 | tf_op jit(solution)/shard_map/ppermute | solution.py:205
  45.5 1.4 %collective-permute-start = (f32[1]{0:T(128)}, f32[1]{0:T(128)}, u32[]{:S(2)}, u32[]{:S(2)}) collective-permute-start(f32[1]{0:T(128)} %param.3), channel_id=1, source_target_pairs={{0,8},{1,9},{2,10},{3,11},{4,12},{5,13},{6,14},{7,15},{8,0},{9,1},... | collective-permute-start | bytes 20 | tf_op jit(solution)/shard_map/ppermute | solution.py:205
  54.1 8.3 %collective-permute-start.14 = (bf16[512,128]{1,0:T(8,128)(2,1)S(1)}, bf16[512,128]{1,0:T(8,128)(2,1)S(1)}, u32[]{:S(2)}, u32[]{:S(2)}) collective-permute-start(bf16[512,128]{1,0:T(8,128)(2,1)S(1)} %get-tuple-element.34.refs_0_), channel_id=1, source_target_pairs={{0,6},{1,7},{2,4},{3,5},{4,2},{5,3},{6,0},{7,1},{8,14},{9,15},{10,... | collective-permute-start | bytes 393224 | tf_op jit(solution)/shard_map/ppermute | solution.py:205
  56.2 11.1 %collective-permute-start.13 = (bf16[512,128]{1,0:T(8,128)(2,1)S(1)}, bf16[512,128]{1,0:T(8,128)(2,1)S(1)}, u32[]{:S(2)}, u32[]{:S(2)}) collective-permute-start(bf16[512,128]{1,0:T(8,128)(2,1)S(1)} %get-tuple-element.34.refs_0_), channel_id=1, source_target_pairs={{0,4},{1,5},{2,6},{3,7},{4,0},{5,1},{6,2},{7,3},{8,12},{9,13},{10,... | collective-permute-start | bytes 393224 | tf_op jit(solution)/shard_map/ppermute | solution.py:205
  56.2 11.1 %collective-permute-start.12 = (bf16[512,128]{1,0:T(8,128)(2,1)S(1)}, bf16[512,128]{1,0:T(8,128)(2,1)S(1)}, u32[]{:S(2)}, u32[]{:S(2)}) collective-permute-start(bf16[512,128]{1,0:T(8,128)(2,1)S(1)} %get-tuple-element.34.refs_0_), channel_id=1, source_target_pairs={{0,2},{1,3},{2,0},{3,1},{4,6},{5,7},{6,4},{7,5},{8,10},{9,11},{10,... | collective-permute-start | bytes 393224 | tf_op jit(solution)/shard_map/ppermute | solution.py:205
  58.6 9.3 %collective-permute-start.22 = (bf16[528,128]{1,0:T(8,128)(2,1)S(1)}, bf16[528,128]{1,0:T(8,128)(2,1)S(1)}, u32[]{:S(2)}, u32[]{:S(2)}) collective-permute-start(bf16[528,128]{1,0:T(8,128)(2,1)S(1)} %get-tuple-element.33.tail_ref), channel_id=1, source_target_pairs={{0,17},{1,16},{2,19},{3,18},{4,21},{5,20},{6,23},{7,22},{8,25},{9,... | collective-permute-start | bytes 405512 | tf_op jit(solution)/shard_map/ppermute | solution.py:205
  60.1 7.9 %collective-permute-start.15 = (bf16[512,128]{1,0:T(8,128)(2,1)S(1)}, bf16[512,128]{1,0:T(8,128)(2,1)S(1)}, u32[]{:S(2)}, u32[]{:S(2)}) collective-permute-start(bf16[512,128]{1,0:T(8,128)(2,1)S(1)} %get-tuple-element.34.refs_0_), channel_id=1, source_target_pairs={{0,8},{1,9},{2,10},{3,11},{4,12},{5,13},{6,14},{7,15},{8,0},{9,1},... | collective-permute-start | bytes 393224 | tf_op jit(solution)/shard_map/ppermute | solution.py:205
  62.4 5.6 %collective-permute-start.18 = (bf16[512,128]{1,0:T(8,128)(2,1)S(1)}, bf16[512,128]{1,0:T(8,128)(2,1)S(1)}, u32[]{:S(2)}, u32[]{:S(2)}) collective-permute-start(bf16[512,128]{1,0:T(8,128)(2,1)S(1)} %collective-permute-done.14.refs_3_), channel_id=1, source_target_pairs={{0,8},{1,9},{2,10},{3,11},{4,12},{5,13},{6,14},{7,15},{8,0},{9,1},... | collective-permute-start | bytes 393224 | tf_op jit(solution)/shard_map/ppermute | solution.py:205
  67.3 1.3 %collective-permute-start.17 = (bf16[512,128]{1,0:T(8,128)(2,1)S(1)}, bf16[512,128]{1,0:T(8,128)(2,1)S(1)}, u32[]{:S(2)}, u32[]{:S(2)}) collective-permute-start(bf16[512,128]{1,0:T(8,128)(2,1)S(1)} %collective-permute-done.13.refs_2_), channel_id=1, source_target_pairs={{0,8},{1,9},{2,10},{3,11},{4,12},{5,13},{6,14},{7,15},{8,0},{9,1},... | collective-permute-start | bytes 393224 | tf_op jit(solution)/shard_map/ppermute | solution.py:205
  67.3 1.5 %collective-permute-start.16 = (bf16[512,128]{1,0:T(8,128)(2,1)S(1)}, bf16[512,128]{1,0:T(8,128)(2,1)S(1)}, u32[]{:S(2)}, u32[]{:S(2)}) collective-permute-start(bf16[512,128]{1,0:T(8,128)(2,1)S(1)} %collective-permute-done.12.refs_1_), channel_id=1, source_target_pairs={{0,8},{1,9},{2,10},{3,11},{4,12},{5,13},{6,14},{7,15},{8,0},{9,1},... | collective-permute-start | bytes 393224 | tf_op jit(solution)/shard_map/ppermute | solution.py:205
  67.9 18.5 %collective-permute-start.26 = (bf16[512,128]{1,0:T(8,128)(2,1)S(1)}, bf16[512,128]{1,0:T(8,128)(2,1)S(1)}, u32[]{:S(2)}, u32[]{:S(2)}) collective-permute-start(bf16[512,128]{1,0:T(8,128)(2,1)S(1)} %shard_map.37.refs_0_), channel_id=1, source_target_pairs={{0,8},{1,9},{2,10},{3,11},{4,12},{5,13},{6,14},{7,15},{8,0},{9,1},... | collective-permute-start | bytes 393224 | tf_op jit(solution)/shard_map/ppermute | solution.py:205
  71.4 25.8 %copy-start.3 = (bf16[224,1024]{1,0:T(8,128)(2,1)S(1)}, bf16[224,1024]{1,0:T(8,128)(2,1)}, u32[]{:S(2)}) copy-start(bf16[224,1024]{1,0:T(8,128)(2,1)} %copy-done.2) | copy-start | bytes 1376260
  72.6 25.8 %copy-start.1 = (bf16[224,1024]{1,0:T(8,128)(2,1)S(1)}, bf16[224,1024]{1,0:T(8,128)(2,1)}, u32[]{:S(2)}) copy-start(bf16[224,1024]{1,0:T(8,128)(2,1)} %copy-done) | copy-start | bytes 1376260
  72.6 27.9 %collective-permute-start.20 = (bf16[224,1024]{1,0:T(8,128)(2,1)S(1)}, bf16[224,1024]{1,0:T(8,128)(2,1)S(1)}, u32[]{:S(2)}, u32[]{:S(2)}) collective-permute-start(bf16[224,1024]{1,0:T(8,128)(2,1)S(1)} %shard_map.36), channel_id=1, source_target_pairs={{0,16},{1,17},{2,18},{3,19},{4,20},{5,21},{6,22},{7,23},{8,24},{9,... | collective-permute-start | bytes 1376264 | tf_op jit(solution)/shard_map/ppermute | solution.py:205
  73.2 27.3 %collective-permute-start.19 = (bf16[224,1024]{1,0:T(8,128)(2,1)S(1)}, bf16[224,1024]{1,0:T(8,128)(2,1)S(1)}, u32[]{:S(2)}, u32[]{:S(2)}) collective-permute-start(bf16[224,1024]{1,0:T(8,128)(2,1)S(1)} %get-tuple-element.36), channel_id=1, source_target_pairs={{0,1},{1,0},{2,3},{3,2},{4,5},{5,4},{6,7},{7,6},{8,9},{9,8},{10,11... | collective-permute-start | bytes 1376264 | tf_op jit(solution)/shard_map/ppermute | solution.py:205
  74.7 11.8 %collective-permute-start.21 = (f32[1]{0:T(128)}, f32[1]{0:T(128)}, u32[]{:S(2)}, u32[]{:S(2)}) collective-permute-start(f32[1]{0:T(128)} %select_n.22), channel_id=1, source_target_pairs={{0,17},{1,16},{2,19},{3,18},{4,21},{5,20},{6,23},{7,22},{8,25},{9,... | collective-permute-start | bytes 20 | tf_op jit(solution)/shard_map/ppermute | solution.py:205
  83.5 8.2 %collective-permute-start.25 = (bf16[512,128]{1,0:T(8,128)(2,1)S(1)}, bf16[512,128]{1,0:T(8,128)(2,1)S(1)}, u32[]{:S(2)}, u32[]{:S(2)}) collective-permute-start(bf16[512,128]{1,0:T(8,128)(2,1)S(1)} %shard_map.37.refs_0_), channel_id=1, source_target_pairs={{0,6},{1,7},{2,4},{3,5},{4,2},{5,3},{6,0},{7,1},{8,14},{9,15},{10,... | collective-permute-start | bytes 393224 | tf_op jit(solution)/shard_map/ppermute | solution.py:205
  86.5 9.5 %collective-permute-start.24 = (bf16[512,128]{1,0:T(8,128)(2,1)S(1)}, bf16[512,128]{1,0:T(8,128)(2,1)S(1)}, u32[]{:S(2)}, u32[]{:S(2)}) collective-permute-start(bf16[512,128]{1,0:T(8,128)(2,1)S(1)} %shard_map.37.refs_0_), channel_id=1, source_target_pairs={{0,4},{1,5},{2,6},{3,7},{4,0},{5,1},{6,2},{7,3},{8,12},{9,13},{10,... | collective-permute-start | bytes 393224 | tf_op jit(solution)/shard_map/ppermute | solution.py:205
  86.5 9.5 %collective-permute-start.23 = (bf16[512,128]{1,0:T(8,128)(2,1)S(1)}, bf16[512,128]{1,0:T(8,128)(2,1)S(1)}, u32[]{:S(2)}, u32[]{:S(2)}) collective-permute-start(bf16[512,128]{1,0:T(8,128)(2,1)S(1)} %shard_map.37.refs_0_), channel_id=1, source_target_pairs={{0,2},{1,3},{2,0},{3,1},{4,6},{5,7},{6,4},{7,5},{8,10},{9,11},{10,... | collective-permute-start | bytes 393224 | tf_op jit(solution)/shard_map/ppermute | solution.py:205
  91.7 6.7 %collective-permute-start.29 = (bf16[512,128]{1,0:T(8,128)(2,1)S(1)}, bf16[512,128]{1,0:T(8,128)(2,1)S(1)}, u32[]{:S(2)}, u32[]{:S(2)}) collective-permute-start(bf16[512,128]{1,0:T(8,128)(2,1)S(1)} %collective-permute-done.25.refs_3_), channel_id=1, source_target_pairs={{0,8},{1,9},{2,10},{3,11},{4,12},{5,13},{6,14},{7,15},{8,0},{9,1},... | collective-permute-start | bytes 393224 | tf_op jit(solution)/shard_map/ppermute | solution.py:205
  96.0 2.4 %collective-permute-start.28 = (bf16[512,128]{1,0:T(8,128)(2,1)S(1)}, bf16[512,128]{1,0:T(8,128)(2,1)S(1)}, u32[]{:S(2)}, u32[]{:S(2)}) collective-permute-start(bf16[512,128]{1,0:T(8,128)(2,1)S(1)} %collective-permute-done.24.refs_2_), channel_id=1, source_target_pairs={{0,8},{1,9},{2,10},{3,11},{4,12},{5,13},{6,14},{7,15},{8,0},{9,1},... | collective-permute-start | bytes 393224 | tf_op jit(solution)/shard_map/ppermute | solution.py:205
  96.0 2.4 %collective-permute-start.27 = (bf16[512,128]{1,0:T(8,128)(2,1)S(1)}, bf16[512,128]{1,0:T(8,128)(2,1)S(1)}, u32[]{:S(2)}, u32[]{:S(2)}) collective-permute-start(bf16[512,128]{1,0:T(8,128)(2,1)S(1)} %collective-permute-done.23.refs_1_), channel_id=1, source_target_pairs={{0,8},{1,9},{2,10},{3,11},{4,12},{5,13},{6,14},{7,15},{8,0},{9,1},... | collective-permute-start | bytes 393224 | tf_op jit(solution)/shard_map/ppermute | solution.py:205
  (5 other events, 54.5 us)
